TPU v7x, 128 devices: a whole 4x4x4 slice. The times are simulated.
128 devices in a mesh: dp: 1, tp: 2 (over core), sp: 64 (over z, y, x).
Axes of the slice: x: 4, y: 4, z: 4, core: 2. Of those that a mesh axis runs over, the one named last changes fastest.
Arguments:
- hidden: bfloat16 [32, 6144], P('dp')
- norm_scale: bfloat16 [6144], replicated
- w_qkv: bfloat16 [6144, 8192], P(None, 'tp')
- w_out: bfloat16 [6144, 6144], P('tp')
- k_cache: bfloat16 [32, 4096, 8, 128], P('dp', 'sp', 'tp')
- v_cache: bfloat16 [32, 4096, 8, 128], P('dp', 'sp', 'tp')
- positions: int32 [32], P('dp')
Outputs:
- output 1: bfloat16 [32, 6144], P('dp')
- output 2: bfloat16 [32, 4096, 8, 128], P('dp', 'sp', 'tp')
- output 3: bfloat16 [32, 4096, 8, 128], P('dp', 'sp', 'tp')
All inputs are finite; a program needn't handle non-finite values.
Results may differ from a plain program's by a relative error of at most 0.00522225.
Values sent between devices are 32-bit elements.
A program may use at most 1 GiB of HBM per device.

v0:
```python
import math
import jax
import jax.numpy as jnp
from jax import lax
from jax.sharding import PartitionSpec as P


def rope_apply(head_vals, positions):
    half_dim = head_vals.shape[-1] // 2
    inv_freq = jnp.exp(jnp.arange(half_dim, dtype=jnp.float32) * (-2.0 * math.log(500000.0) / head_vals.shape[-1]))
    angles = positions.astype(jnp.float32)[:, None] * inv_freq[None, :]
    cos_part = jnp.cos(angles)[:, None, None, :]
    sin_part = jnp.sin(angles)[:, None, None, :]
    first_half = head_vals[..., :half_dim]
    second_half = head_vals[..., half_dim:]
    return jnp.concatenate([first_half * cos_part - second_half * sin_part, second_half * cos_part + first_half * sin_part], axis=-1)


def layer_norm_bf16(hidden_f32, norm_scale):
    row_mean = jnp.mean(hidden_f32, axis=-1, keepdims=True)
    centered = hidden_f32 - row_mean
    row_var = jnp.mean(centered * centered, axis=-1, keepdims=True)
    return (centered * lax.rsqrt(row_var + 1e-5) * norm_scale.astype(jnp.float32)).astype(jnp.bfloat16)


def solution(mesh):
    cache_spec = P('dp', 'sp', 'tp', None)

    def local_step(hidden, norm_scale, w_qkv, w_out, k_cache, v_cache, positions):
        n_seq, seq_local, kv_local, head_dim = k_cache.shape
        q_per_kv = w_qkv.shape[1] // (kv_local * head_dim) - 2
        hidden_f32 = hidden.astype(jnp.float32)
        normed = layer_norm_bf16(hidden_f32, norm_scale)
        qkv_proj = jnp.clip(jnp.dot(normed, w_qkv, preferred_element_type=jnp.float32).astype(jnp.bfloat16), -8.0, 8.0)
        grouped = qkv_proj.reshape(n_seq, kv_local, q_per_kv + 2, head_dim)
        rotated = rope_apply(grouped[:, :, : q_per_kv + 1].astype(jnp.float32), positions).astype(jnp.bfloat16)
        queries = rotated[:, :, :q_per_kv]
        row_index = lax.axis_index('sp') * seq_local + jnp.arange(seq_local)
        new_row = (row_index[None, :] == positions[:, None])[:, :, None, None]
        k_upd = jnp.where(new_row, rotated[:, :, q_per_kv][:, None], k_cache)
        v_upd = jnp.where(new_row, grouped[:, :, q_per_kv + 1][:, None], v_cache)
        scores = jnp.einsum('bgqd,bsgd->bgqs', queries, k_upd, preferred_element_type=jnp.float32) * (head_dim ** -0.5)
        valid_mask = row_index[None, :] <= positions[:, None]
        scores = jnp.where(valid_mask[:, None, None, :], scores, -1e30)
        local_max = jnp.max(scores, axis=-1)
        weights = jnp.exp(scores - local_max[..., None])
        local_sum = jnp.sum(weights, axis=-1)
        local_out = jnp.einsum('bgqs,bsgd->bgqd', weights.astype(jnp.bfloat16), v_upd, preferred_element_type=jnp.float32)
        global_max = lax.pmax(local_max, 'sp')
        factor = jnp.exp(local_max - global_max)
        packed = jnp.concatenate([local_out * factor[..., None], (local_sum * factor)[..., None]], axis=-1)
        merged = lax.psum(packed, 'sp')
        attn_out = merged[..., :head_dim] / merged[..., head_dim:]
        attn_flat = attn_out.reshape(n_seq, kv_local * q_per_kv * head_dim).astype(jnp.bfloat16)
        head_part = jnp.dot(attn_flat, w_out, preferred_element_type=jnp.float32)
        proj_sum = lax.psum(head_part, 'tp')
        h_out = (hidden_f32 + proj_sum).astype(jnp.bfloat16)
        return h_out, k_upd, v_upd

    return jax.shard_map(
        local_step,
        mesh=mesh,
        in_specs=(P('dp', None), P(None), P(None, 'tp'), P('tp', None), cache_spec, cache_spec, P('dp')),
        out_specs=(P('dp', None), cache_spec, cache_spec),
        check_vma=False,
    )
```

profile of v0, /device:TPU:1, one launch (start us, length us, event | category | flops | bytes accessed | tf_op | source)
XLA Modules:
  0.0 571.3 jit_solution(5965068566700795088)
XLA Ops:
  7.2 0.0 all-reduce.3.cloned.1.call-start
  7.2 1.2 convert_reduce_fusion
  8.4 1.3 fusion.17
  9.7 0.7 convert_element_type.36
  10.4 0.0 copy-start.4
  10.4 20.0 %fusion.14 = bf16[4,8,32,128]{3,1,2,0:T(8,128)(2,1)S(1)} fusion(bf16[6144,4096]{1,0:T(8,128)(2,1)} %param.9, bf16[32,6144]{1,0:T(8,128)(2,1)} %param.7, f32[6144]{0:T(1024)S(1)} %convert_element_type.36, f32[32]{0:T(128)S(1)} %add_rsqrt_fusion, f32[32]{0:T(128)S(1)} %broadcast_multiply_fusion), kind=kOutput, calls=%fused_computation.14 | convolution fusion | flops 1611857920 | bytes 51011840 | tf_op jit(solution)/shard_map/dot_general | solution.py:34
  30.4 0.0 copy-start.1
  30.4 0.1 slice.37
  30.5 0.1 slice_convert_fusion
  30.6 0.0 copy-done.4
  30.6 0.1 broadcast_compare_fusion.1
  30.7 0.1 multiply_cosine_fusion
  30.9 0.2 subtract_convert_fusion
  31.1 0.3 pad_maximum_fusion.1
  31.4 0.6 copy-done.1
  32.0 6.9 %broadcast_select_fusion = (bf16[32,64,4,128]{3,2,1,0:T(4,128)(2,1)}, bf16[32,64,4,128]{3,2,1,0:T(4,128)(2,1)S(1)}) fusion(bf16[32,64,4,128]{3,2,1,0:T(4,128)(2,1)S(1)} %copy-done.1, pred[32,64]{1,0:T(8,128)(4,1)S(1)} %get-tuple-element.10, bf16[32,4,128]{2,1,0:T(4,128)(2,1)S(1)} %copy.27, bf16[32,64,4,128]{3,2,1,0:T(4,128)(2,1)} %param.11, ...), kind=kLoop, calls=%fused_computation.6 | loop fusion | flops 2097152 | bytes 8456192 | tf_op jit(solution)/shard_map/jit(_where)/select_n | solution.py:41
  38.9 0.0 copy-start.3
  38.9 1.3 copy-done.3
  40.2 0.0 copy-start.2
  40.2 1.4 fusion.36
  41.6 296.4 %pmax.7 = f32[32,4,6]{2,1,0:T(4,128)S(1)} all-reduce(f32[32,4,6]{2,1,0:T(4,128)S(1)} %get-tuple-element.13), channel_id=1, replica_groups=mesh['dp'=1,'tp'=2,'sp'=64] {'sp'}, use_global_device_ids=true, to_apply=%region_3.4 | all-reduce | flops 768 | bytes 6144 | tf_op jit(solution)/shard_map/pmax | solution.py:49
  338.0 0.4 fusion.22
  338.5 0.9 copy.30
  339.3 0.0 copy-done.2
  339.3 0.7 fusion.11
  340.1 1.2 pad_maximum_fusion
  341.2 0.0 all-reduce.3.cloned.1.call-update
  341.3 0.0 all-reduce.5.cloned.1.call-start
  341.3 177.6 %all-reduce.3.cloned.1.call-done = f32[32,4,6,129]{3,2,1,0:T(8,128)} async-done(((f32[32,4,6,129]{3,2,1,0:T(8,128)}), f32[32,4,6,129]{3,2,1,0:T(8,128)}) %all-reduce.3.cloned.1.call-update) | async-done | bytes 396304 | tf_op jit(solution)/shard_map/psum | solution.py:52
  518.9 1.1 slice.39
  520.0 0.9 copy.35
  520.8 1.3 fusion.21
  522.1 0.2 convert_element_type.43
  522.3 0.0 copy-start
  522.4 16.0 %fusion.37 = f32[32,6144]{1,0:T(8,128)} fusion(bf16[32,3072]{1,0:T(8,128)(2,1)S(1)} %convert_element_type.43, bf16[3072,6144]{1,0:T(8,128)(2,1)} %param.10), kind=kOutput, calls=%fused_computation.54 | convolution fusion | flops 1207959552 | bytes 38731776 | tf_op jit(solution)/shard_map/dot_general | solution.py:55
  538.4 0.0 all-reduce.5.cloned.1.call-update
  538.4 24.1 %all-reduce.5.cloned.1.call-done = f32[32,6144]{1,0:T(8,128)} async-done(((f32[32,6144]{1,0:T(8,128)}), f32[32,6144]{1,0:T(8,128)}) %all-reduce.5.cloned.1.call-update) | async-done | bytes 786448 | tf_op jit(solution)/shard_map/psum | solution.py:56
  562.5 0.0 copy-done
  562.5 1.9 fusion.20
  (11 shorter events, 0.2 us)
Async XLA Ops:
  7.2 511.7 %all-reduce.3.cloned.1.call-start = ((), (), s32[]{:S(2)}) async-start(), calls=%async_computation | async-start | bytes 2097152 | tf_op jit(solution)/shard_map/psum | solution.py:52
  10.4 20.2 %copy-start.4 = (s32[32]{0:T(128)S(1)}, s32[32]{0:T(128)}, u32[]{:S(2)}) copy-start(s32[32]{0:T(128)} %param.13) | copy-start | bytes 388
  30.4 1.6 copy-start.1
  38.9 1.3 copy-start.3
  40.2 299.1 %copy-start.2 = (bf16[32,64,4,128]{3,2,1,0:T(4,128)(2,1)S(1)}, bf16[32,64,4,128]{3,2,1,0:T(4,128)(2,1)}, u32[]{:S(2)}) copy-start(bf16[32,64,4,128]{3,2,1,0:T(4,128)(2,1)} %get-tuple-element.7) | copy-start | bytes 6291460
  341.3 221.3 %all-reduce.5.cloned.1.call-start = ((), (), s32[]{:S(2)}) async-start(), calls=%async_computation.1 | async-start | bytes 1572864 | tf_op jit(solution)/shard_map/psum | solution.py:56
  522.3 40.2 %copy-start = (bf16[32,6144]{1,0:T(8,128)(2,1)S(1)}, bf16[32,6144]{1,0:T(8,128)(2,1)}, u32[]{:S(2)}) copy-start(bf16[32,6144]{1,0:T(8,128)(2,1)} %param.7) | copy-start | bytes 1179652
Sparse Core Ops, SparseCore 0:
  341.4 177.4 all-reduce.2
  538.5 23.9 all-reduce.4
where the time goes:
time: 572 us; the launch traced here: 571 us
  blocking collectives  296 us (52%)
  waiting for transfers between devices  202 us (35%)
  matrix products  38.1 us (7%)
  other arithmetic  15.7 us (3%)
  between operations  14.2 us (2%)
    pmax x1, blocking collectives, local_step(): global_max = lax.pmax(local_max, 'sp')  296 us
    psum x1, waiting for transfers between devices, local_step(): merged = lax.psum(packed, 'sp')  178 us
    psum x1, waiting for transfers between devices, local_step(): proj_sum = lax.psum(head_part, 'tp')  24.1 us
    dot_general x1, matrix products, local_step(): jnp.dot(normed, w_qkv, preferred_element_type=jnp.float32)  20 us
    dot_general x1, matrix products, local_step(): head_part = jnp.dot(attn_flat, w_out, preferred_element_type=jnp.float32)  16 us
  transfers between devices with their start and end apart: 2, of which 2 were waited for; matrix products, arithmetic and copies ran while one was open for 0% of the time, Pallas kernels for 0%

commit v1 on v0

v1 whole, which is shorter than its diff:
```python
import functools
import math

import jax
import jax.numpy as jnp
from jax import lax
from jax.experimental import pallas as pl
from jax.experimental.pallas import tpu as pltpu
from jax.sharding import PartitionSpec as P

MESH = pl.DeviceIdType.MESH
VMEM = pltpu.VMEM
F32 = jnp.float32
BF16 = jnp.bfloat16
NEG = -3.0e38
PLANE = 16
K_CHUNKS = 6


def qkv_kernel(h_ref, scale_ref, cos_ref, sin_ref, w_ref, x_ref,
               w_buf, recv, xs, w_sem, send_sem, recv_sem):
    sp = lax.axis_index("sp")
    j = lax.rem(sp, PLANE)
    base = sp - j
    n_seq, d_model = h_ref.shape
    width = w_buf.shape[1]
    rows = d_model // K_CHUNKS
    cols = pl.ds(pl.multiple_of(j * width, width), width)

    def w_copy(c):
        return pltpu.make_async_copy(
            w_ref.at[pl.ds(c * rows, rows), cols], w_buf.at[pl.ds(c * rows, rows)], w_sem.at[c])

    for c in range(K_CHUNKS):
        w_copy(c).start()
    barrier = pltpu.get_barrier_semaphore()

    def greet(d, carry):
        pl.semaphore_signal(barrier, inc=1, device_id={"sp": base + lax.rem(j + d, PLANE)}, device_id_type=MESH)
        return carry

    lax.fori_loop(1, PLANE, greet, 0)

    hidden = h_ref[...].astype(F32)
    centered = hidden - jnp.mean(hidden, axis=-1, keepdims=True)
    var = jnp.mean(centered * centered, axis=-1, keepdims=True)
    u = (centered * lax.rsqrt(var + 1e-5) * scale_ref[...].astype(F32)).astype(BF16)
    acc = jnp.zeros((n_seq, width), F32)
    for c in range(K_CHUNKS):
        w_copy(c).wait()
        acc += jnp.dot(u[:, c * rows:(c + 1) * rows], w_buf[c * rows:(c + 1) * rows, :],
                       preferred_element_type=F32)
    y = jnp.clip(acc.astype(BF16), -8.0, 8.0).astype(F32)
    heads = []
    is_kv = lax.rem(j, 4) == 3
    for i in range(width // 128):
        part = y[:, i * 128:(i + 1) * 128]
        swapped = pltpu.roll(part, 64, 1)
        turned = (part * cos_ref[...] + swapped * sin_ref[...]).astype(BF16).astype(F32)
        heads.append(turned if i == 0 else jnp.where(is_kv, part, turned))
    recv[j] = jnp.concatenate(heads, axis=1)
    pl.semaphore_wait(barrier, PLANE - 1)

    def send(d):
        return pltpu.make_async_remote_copy(
            src_ref=recv.at[j], dst_ref=recv.at[j], send_sem=send_sem, recv_sem=recv_sem,
            device_id={"sp": base + lax.rem(j + d, PLANE)}, device_id_type=MESH)

    def start(d, carry):
        send(d).start()
        return carry

    lax.fori_loop(1, PLANE, start, 0)
    others = recv.at[pl.ds(0, PLANE - 1)]
    pltpu.make_async_copy(others, others, recv_sem).wait()
    for blk in range(PLANE):
        for i in range(width // 128):
            xs[pl.ds(blk * (width // 128) + i, n_seq, stride=32), :] = recv[blk, :, i * 128:(i + 1) * 128]
    x_ref[...] = xs[...].astype(BF16)
    pltpu.make_async_copy(others, others, send_sem).wait()


def attn_kernel(pos_ref, x_ref, k_ref, v_ref, o_ref, k_out, v_out, k_buf, v_buf, in_sem, out_sem):
    n_seq, n_rows, head_dim = k_ref.shape
    kv = 4
    seq_local = n_rows // kv
    base = lax.axis_index("sp") * seq_local
    steps, per = 8, n_seq // 8

    def load(c, which):
        src, dst = ((k_ref, k_buf), (v_ref, v_buf))[which]
        return pltpu.make_async_copy(src.at[pl.ds(c * per, per)], dst.at[pl.ds(c * per, per)], in_sem.at[which, c])

    def store(c, which):
        src, dst = ((k_buf, k_out), (v_buf, v_out))[which]
        return pltpu.make_async_copy(src.at[pl.ds(c * per, per)], dst.at[pl.ds(c * per, per)], out_sem.at[which, c])

    for c in range(steps):
        load(c, 0).start()
        load(c, 1).start()
    row = lax.broadcasted_iota(jnp.int32, (32, n_rows), 0)
    col = lax.broadcasted_iota(jnp.int32, (32, n_rows), 1)
    seq_of = jnp.where(col % kv == row // 8, col // kv + base, 1 << 30)
    row8 = lax.broadcasted_iota(jnp.int32, (32, head_dim), 0) % 8
    diag = lax.broadcasted_iota(jnp.int32, (32, head_dim), 1) == row8
    slab_row = lax.broadcasted_iota(jnp.int32, (n_rows, head_dim), 0)
    scale = head_dim ** -0.5

    def spread(col_vec):
        tiles = jnp.where(diag, col_vec, 0.0).reshape(4, 8, head_dim)
        return jnp.broadcast_to(jnp.sum(tiles, axis=1, keepdims=True), (4, 8, head_dim)).reshape(32, head_dim)

    for c in range(steps):
        load(c, 0).wait()
        load(c, 1).wait()
        for i in range(per):
            b = c * per + i
            p = pos_ref[b]
            xb = x_ref[pl.ds(b * 32, 32), :]

            @pl.when(jnp.logical_and(p >= base, p < base + seq_local))
            def _():
                xf = xb.astype(F32)
                for buf, r in ((k_buf, 6), (v_buf, 7)):
                    new = jnp.zeros((n_rows, head_dim), F32)
                    for g in range(kv):
                        new = jnp.where(slab_row % kv == g, xf[g * 8 + r:g * 8 + r + 1, :], new)
                    buf[b] = jnp.where(slab_row // kv + base == p, new, buf[b].astype(F32)).astype(BF16)

            s = lax.dot_general(xb, k_buf[b], (((1,), (1,)), ((), ())), preferred_element_type=F32) * scale
            s = jnp.where(seq_of <= p, s, NEG)
            m = jnp.max(s, axis=1, keepdims=True)
            e = jnp.exp(s - m)
            l = jnp.sum(e, axis=1, keepdims=True)
            o = jnp.dot(e.astype(BF16), v_buf[b], preferred_element_type=F32)
            o = jnp.where(row8 == 6, spread(m), jnp.where(row8 == 7, spread(l), o))
            o_ref[pl.ds(b * 4, 4)] = o.reshape(4, 8, head_dim)
        store(c, 0).start()
        store(c, 1).start()
    for c in range(steps):
        store(c, 0).wait()
        store(c, 1).wait()


def merge_kernel(n_sp, o_ref, h_ref, w_ref, out_ref, parts, w_buf, lhs, mine, shares, full, other,
                 w_sem, rs_send, rs_recv, x_send, x_recv, ag_send, ag_recv, tp_send, tp_recv):
    sp = lax.axis_index("sp")
    tp = lax.axis_index("tp")
    line, group = lax.div(sp, 4), lax.rem(sp, 4)
    depth = w_buf.shape[0]
    width = 768
    n_own = 8

    def w_copy(c):
        return pltpu.make_async_copy(
            w_ref.at[pl.ds(pl.multiple_of(group * depth, depth), depth), pl.ds(c * width, width)],
            w_buf.at[:, pl.ds(c * width, width)], w_sem.at[c])

    for c in range(n_own):
        w_copy(c).start()

    barrier = pltpu.get_barrier_semaphore()

    def greet(d, carry):
        pl.semaphore_signal(barrier, inc=1, device_id={"sp": lax.rem(sp + d, n_sp)}, device_id_type=MESH)
        return carry

    lax.fori_loop(1, n_sp, greet, 0)
    for d in range(4):
        pl.semaphore_signal(barrier, inc=1, device_id={"tp": 1 - tp, "sp": line * 4 + lax.rem(group + d, 4)},
                            device_id_type=MESH)
    pl.semaphore_wait(barrier, n_sp - 1 + 4)

    def rs(d):
        peer = lax.rem(sp + d, n_sp)
        return pltpu.make_async_remote_copy(
            src_ref=o_ref.at[lax.div(peer, 4), :, lax.rem(peer, 4)], dst_ref=parts.at[sp], send_sem=rs_send,
            recv_sem=rs_recv, device_id={"sp": peer}, device_id_type=MESH)

    def rs_start(d, carry):
        rs(d).start()
        return carry

    lax.fori_loop(1, n_sp, rs_start, 0)
    parts[sp] = o_ref[line, :, group]
    others = parts.at[pl.ds(0, n_sp - 1)]
    pltpu.make_async_copy(others, others, rs_recv).wait()

    lane = lax.broadcasted_iota(jnp.int32, (1, 128), 1)
    lhs[...] = jnp.zeros_like(lhs)
    for t in range(2):
        m = parts[:, t, 6, :]
        l = parts[:, t, 7, :]
        f = jnp.exp(m - jnp.max(m, axis=0, keepdims=True))
        den = jnp.sum(f * l, axis=0, keepdims=True)
        wt = (f / jnp.where(lane < 6, den, 1.0)).T
        acc = jnp.zeros((8, 128), F32)
        for s in range(n_sp):
            acc += wt[:8, s:s + 1] * parts[s, t]
        for hd in range(6):
            lhs[t:t + 1, hd * 128:(hd + 1) * 128] = acc[hd:hd + 1, :]

    me = group * 2 + tp
    left = lhs[...].astype(BF16)
    for c in range(n_own):
        w_copy(c).wait()
        res = jnp.dot(left, w_buf[:, c * width:(c + 1) * width], preferred_element_type=F32)
        for t in range(2):
            for cb in range(6):
                mine[c, t, cb:cb + 1, :] = res[t:t + 1, cb * 128:(cb + 1) * 128]

    def x_copy(d):
        owner = lax.rem(me + d, n_own)
        return pltpu.make_async_remote_copy(
            src_ref=mine.at[owner], dst_ref=shares.at[me], send_sem=x_send, recv_sem=x_recv,
            device_id={"tp": lax.rem(owner, 2), "sp": line * 4 + lax.div(owner, 2)}, device_id_type=MESH)

    for d in range(1, n_own):
        x_copy(d).start()
    shares[me] = mine[me]
    x_others = shares.at[pl.ds(0, n_own - 1)]
    pltpu.make_async_copy(x_others, x_others, x_recv).wait()
    slot = group * (n_sp // 4) + line
    total = shares[0]
    for s in range(1, n_own):
        total += shares[s]
    full[slot] = total

    def ag(d):
        return pltpu.make_async_remote_copy(
            src_ref=full.at[slot], dst_ref=full.at[slot], send_sem=ag_send, recv_sem=ag_recv,
            device_id={"sp": lax.rem(sp + d, n_sp)}, device_id_type=MESH)

    def ag_start(d, carry):
        ag(d).start()
        return carry

    lax.fori_loop(1, n_sp, ag_start, 0)
    f_others = full.at[pl.ds(0, n_sp - 1)]
    pltpu.make_async_copy(f_others, f_others, ag_recv).wait()
    swap = pltpu.make_async_remote_copy(
        src_ref=full, dst_ref=other, send_sem=tp_send, recv_sem=tp_recv, device_id={"tp": 1 - tp},
        device_id_type=MESH)
    swap.start()

    def finish(buf, core):
        for g in range(4):
            for cb in range(6):
                slab = jnp.concatenate(
                    [buf[pl.ds(g * 16 + q * 4, 4), :, cb, :].reshape(8, 128) for q in range(4)], axis=0)
                at = pl.ds(pl.multiple_of((g * 2 + core) * width + cb * 128, 128), 128)
                out_ref[:, at] = (h_ref[:, at].astype(F32) + slab).astype(BF16)

    finish(full, tp)
    swap.wait()
    finish(other, 1 - tp)
    pltpu.make_async_copy(others, others, rs_send).wait()
    pltpu.make_async_copy(x_others, x_others, x_send).wait()
    pltpu.make_async_copy(f_others, f_others, ag_send).wait()


def solution(mesh):
    cache_spec = P('dp', 'sp', 'tp', None)
    n_sp = mesh.shape["sp"]

    def local_step(hidden, norm_scale, w_qkv, w_out, k_cache, v_cache, positions):
        n_seq, seq_local, kv, head_dim = k_cache.shape
        d_model = hidden.shape[1]
        width = w_qkv.shape[1] // PLANE
        vmem = pl.BlockSpec(memory_space=VMEM)
        anyspace = pl.BlockSpec(memory_space=pl.ANY)
        half = head_dim // 2
        inv_freq = jnp.exp(jnp.arange(half, dtype=F32) * (-2.0 * math.log(500000.0) / head_dim))
        angles = positions.astype(F32)[:, None] * inv_freq[None, :]
        cos, sin = jnp.cos(angles), jnp.sin(angles)
        cos = jnp.concatenate([cos, cos], axis=1)
        sin = jnp.concatenate([-sin, sin], axis=1)

        x = pl.pallas_call(
            qkv_kernel,
            out_shape=jax.ShapeDtypeStruct((n_seq * 32, head_dim), BF16),
            in_specs=[vmem, vmem, vmem, vmem, anyspace],
            out_specs=vmem,
            scratch_shapes=[
                VMEM((d_model, width), BF16),
                VMEM((PLANE, n_seq, width), F32),
                VMEM((n_seq * 32, head_dim), F32),
                pltpu.SemaphoreType.DMA((K_CHUNKS,)),
                pltpu.SemaphoreType.DMA,
                pltpu.SemaphoreType.DMA,
            ],
            compiler_params=pltpu.CompilerParams(collective_id=0, has_side_effects=True),
            name="qkv",
        )(hidden, norm_scale.reshape(1, d_model), cos, sin, w_qkv)

        rows = seq_local * kv
        flat = (n_seq, rows, head_dim)
        o, k_new, v_new = pl.pallas_call(
            attn_kernel,
            out_shape=[
                jax.ShapeDtypeStruct((n_seq * kv, 8, head_dim), F32),
                jax.ShapeDtypeStruct(flat, BF16),
                jax.ShapeDtypeStruct(flat, BF16),
            ],
            in_specs=[pl.BlockSpec(memory_space=pltpu.SMEM), vmem, anyspace, anyspace],
            out_specs=[vmem, anyspace, anyspace],
            scratch_shapes=[
                VMEM(flat, BF16),
                VMEM(flat, BF16),
                pltpu.SemaphoreType.DMA((2, 8)),
                pltpu.SemaphoreType.DMA((2, 8)),
            ],
            name="attn",
        )(positions, x, k_cache.reshape(flat), v_cache.reshape(flat))

        depth = w_out.shape[0] // kv
        h_out = pl.pallas_call(
            functools.partial(merge_kernel, n_sp),
            out_shape=jax.ShapeDtypeStruct((n_seq, d_model), BF16),
            in_specs=[vmem, vmem, anyspace],
            out_specs=vmem,
            scratch_shapes=[
                VMEM((n_sp, 2, 8, head_dim), F32),
                VMEM((depth, d_model), BF16),
                VMEM((8, depth), F32),
                VMEM((8, 2, 8, head_dim), F32),
                VMEM((8, 2, 8, head_dim), F32),
                VMEM((n_sp, 2, 8, head_dim), F32),
                VMEM((n_sp, 2, 8, head_dim), F32),
                pltpu.SemaphoreType.DMA((8,)),
            ] + [pltpu.SemaphoreType.DMA] * 8,
            compiler_params=pltpu.CompilerParams(collective_id=1, has_side_effects=True),
            name="merge",
        )(o.reshape(n_seq // 2, 2, kv, 8, head_dim), hidden, w_out)
        return h_out, k_new.reshape(k_cache.shape), v_new.reshape(v_cache.shape)

    return jax.shard_map(
        local_step,
        mesh=mesh,
        in_specs=(P('dp', None), P(None), P(None, 'tp'), P('tp', None), cache_spec, cache_spec, P('dp')),
        out_specs=(P('dp', None), cache_spec, cache_spec),
        check_vma=False,
    )
```

time: 572 us -> 74.6 us (0.13)
  blocking collectives: 296 us -> 0 us
  waiting for transfers between devices: 202 us -> 0 us
  Pallas kernels: 0 us -> 69.2 us
  matrix products: 38.1 us -> 0 us
  other arithmetic: 15.7 us -> 1.5 us
  between operations: 14.2 us -> 0.66 us
    pmax x1 -> x0, blocking collectives: 296 us -> none  [local_step(): global_max = lax.pmax(local_max, 'sp')]
    psum x2 -> x0, waiting for transfers between devices: 202 us -> none  [the longest x1 178 us: local_step(): merged = lax.psum(packed, 'sp')]
    pallas_call x0 -> x3, Pallas kernels: none -> 69.2 us  [the longest x1 37.1 us: local_step(): pl.pallas_call(functools.partial(merge_kernel, n_sp), out_shape=jax.Shape...]
    dot_general x4 -> x0, matrix products: 38.1 us -> none  [the longest x1 20 us: local_step(): jnp.dot(normed, w_qkv, preferred_element_type=jnp.float32)]
    select_n x1 -> x0, other arithmetic: 6.94 us -> none  [local_step(): v_upd = jnp.where(new_row, grouped[:, :, q_per_kv + 1][:, None], v_cache)]
  transfers between devices with their start and end apart: 2 -> 0, of which waited for: 2 -> 0; matrix products, arithmetic and copies ran while one was open for 0% -> 0% of each run, Pallas kernels for 0% -> 0%
where the time goes in v1:
time: 74.6 us; the launch traced here: 74.4 us
  Pallas kernels  69.2 us (93%)
  local copies, waits for them, and re-layouts  3.1 us (4%)
  other arithmetic  1.5 us (2%)
    pallas_call x1, Pallas kernels, local_step(): pl.pallas_call(functools.partial(merge_kernel, n_sp), out_shape=jax.Shape...  37.1 us
    pallas_call x1, Pallas kernels, local_step(): pl.pallas_call(qkv_kernel, out_shape=jax.ShapeDtypeStruct((n_seq * 32, he...  17 us
    pallas_call x1, Pallas kernels, local_step(): pl.pallas_call(attn_kernel, out_shape=[jax.ShapeDtypeStruct((n_seq * kv,...  15 us
    unnamed x1, local copies, waits for them, and re-layouts  1.77 us

profile of v1, /device:TPU:1, one launch (start us, length us, event | category | flops | bytes accessed | tf_op | source)
XLA Modules:
  0.0 74.4 jit_solution(732679045908076732)
XLA Ops:
  0.6 0.7 convert_element_type.3
  1.3 1.3 %reshape.30.scale_ref = bf16[1,6144]{1,0:T(2,128)(2,1)} reshape(bf16[6144]{0:T(1024)(128)(2,1)} %param.8) | data formatting | bytes 24576 | tf_op jit(solution)/shard_map/reshape | solution.py:294
  2.6 0.1 fusion
  2.8 0.7 pad_maximum_fusion
  3.5 17.0 %qkv.1.x_ref = bf16[1024,128]{1,0:T(8,128)(2,1)} custom-call(bf16[32,6144]{1,0:T(8,128)(2,1)} %h_ref.3, bf16[1,6144]{1,0:T(2,128)(2,1)} %reshape.30.scale_ref, f32[32,128]{1,0:T(8,128)} %get-tuple-element.12.cos_ref, f32[32,128]{1,0:T(8,128)} %get-tuple-element.13.sin_ref, bf16[6144,4096]{1,0:T(8,128)(2,1)} %w_ref.2), custom_call_target="tpu_custom_call" | custom-call | tf_op jit(solution)/shard_map/qkv/pallas_call | solution.py:279
  20.5 15.0 %attn.1 = (f32[128,8,128]{2,1,0:T(8,128)}, bf16[32,256,128]{2,1,0:T(8,128)(2,1)}, bf16[32,256,128]{2,1,0:T(8,128)(2,1)}) custom-call(s32[32]{0:T(128)} %pos_ref.1, bf16[1024,128]{1,0:T(8,128)(2,1)} %qkv.1.x_ref, bf16[32,256,128]{2,1,0:T(8,128)(2,1)} %bitcast.5, bf16[32,256,128]{2,1,0:T(8,128)(2,1)} %bitcast.6), custom_call_target="tpu_custom_call" | custom-call | tf_op jit(solution)/shard_map/attn/pallas_call | solution.py:298
  35.6 37.1 %merge.1 = bf16[32,6144]{1,0:T(8,128)(2,1)} custom-call(f32[16,2,4,8,128]{4,3,2,1,0:T(8,128)} %bitcast.7, bf16[32,6144]{1,0:T(8,128)(2,1)} %h_ref.3, bf16[3072,6144]{1,0:T(8,128)(2,1)} %w_ref.3), custom_call_target="tpu_custom_call" | custom-call | tf_op jit(solution)/shard_map/merge/pallas_call | solution.py:317
  72.7 1.8 %copy.11 = bf16[32,6144]{1,0:T(8,128)(2,1)} copy(bf16[32,6144]{1,0:T(8,128)(2,1)} %merge.1) | data formatting | bytes 786432
  (1 shorter events, 0.0 us)

commit v2 on v0

v2 whole, which is shorter than its diff:
```python
import functools
import math

import jax
import jax.numpy as jnp
import numpy as np
from jax import lax
from jax.experimental import pallas as pl
from jax.experimental.pallas import tpu as pltpu
from jax.sharding import PartitionSpec as P

MESH = pl.DeviceIdType.MESH
VMEM = pltpu.VMEM
F32 = jnp.float32
BF16 = jnp.bfloat16
NEG = -3.0e38
PLANE = 16
K_CHUNKS = 6
KV = 4
OWNERS = 8


def step_kernel(pos_hbm, h_hbm, scale_hbm, freq_hbm, wq_ref, wo_ref, k_ref, v_ref, out_ref, new_ref,
                pos_ref, h_ref, scale_ref, freq_ref, in_sem, wq_buf, wo_buf, k_buf, v_buf, recv, xs, xb, part, parts, lhs, mine, shares, full, other,
                wq_sem, wo_sem, kv_sem, q_send, q_recv, rs_send, rs_recv, x_send, x_recv,
                ag_send, ag_recv, tp_send, tp_recv):
    sp = lax.axis_index("sp")
    tp = lax.axis_index("tp")
    n_sp = 64
    line, group = lax.div(sp, KV), lax.rem(sp, KV)
    n_lines = n_sp // KV
    j = lax.rem(sp, PLANE)
    base = sp - j
    n_seq, d_model = h_ref.shape
    width = wq_buf.shape[1]
    heads_per = width // 128
    rows = d_model // K_CHUNKS
    n_rows = k_ref.shape[1]
    seq_local = n_rows // KV
    depth = wo_buf.shape[0]
    own = d_model // OWNERS
    n_cb = own // 128

    def wq_copy(c):
        return pltpu.make_async_copy(
            wq_ref.at[pl.ds(c * rows, rows), pl.ds(pl.multiple_of(j * width, width), width)],
            wq_buf.at[pl.ds(c * rows, rows)], wq_sem.at[c])

    def wo_copy(c):
        return pltpu.make_async_copy(
            wo_ref.at[pl.ds(pl.multiple_of(group * depth, depth), depth), pl.ds(c * own, own)],
            wo_buf.at[:, pl.ds(c * own, own)], wo_sem.at[c])

    k_copy = pltpu.make_async_copy(k_ref, k_buf, kv_sem.at[0])
    v_copy = pltpu.make_async_copy(v_ref, v_buf, kv_sem.at[1])
    small = [pltpu.make_async_copy(src, dst, in_sem.at[i]) for i, (src, dst) in enumerate(
        [(h_hbm, h_ref), (pos_hbm, pos_ref), (freq_hbm, freq_ref), (scale_hbm, scale_ref)])]
    for c in small:
        c.start()
    for c in range(K_CHUNKS):
        wq_copy(c).start()
    k_copy.start()
    v_copy.start()
    for c in range(OWNERS):
        wo_copy(c).start()

    barrier = pltpu.get_barrier_semaphore()

    def greet(d, carry):
        pl.semaphore_signal(barrier, inc=1, device_id={"sp": lax.rem(sp + d, n_sp)}, device_id_type=MESH)
        return carry

    with jax.named_scope("greet"):
        lax.fori_loop(1, n_sp, greet, 0)
        for d in range(KV):
            pl.semaphore_signal(barrier, inc=1, device_id={"tp": 1 - tp, "sp": line * KV + lax.rem(group + d, KV)},
                                device_id_type=MESH)

    with jax.named_scope("inwait"):
        for c in small:
            c.wait()
    with jax.named_scope("norm"):
        seq_row = lax.broadcasted_iota(jnp.int32, (n_seq, 128), 0)
        pos = jnp.zeros((n_seq, 128), jnp.int32)
        for b in range(n_seq):
            pos = jnp.where(seq_row == b, pos_ref[b], pos)
        angles = pos.astype(F32) * freq_ref[...]
        cos = jnp.cos(angles)
        sin = jnp.sin(angles)
        sin = jnp.where(lax.broadcasted_iota(jnp.int32, (n_seq, 128), 1) < 64, -sin, sin)
        hidden = h_ref[...].astype(F32)
        centered = hidden - jnp.mean(hidden, axis=-1, keepdims=True)
        var = jnp.mean(centered * centered, axis=-1, keepdims=True)
        u = (centered * lax.rsqrt(var + 1e-5) * scale_ref[...].astype(F32)[None, :]).astype(BF16)

    with jax.named_scope("qkv"):
        acc = jnp.zeros((n_seq, width), F32)
        for c in range(K_CHUNKS):
            wq_copy(c).wait()
            acc += jnp.dot(u[:, c * rows:(c + 1) * rows], wq_buf[c * rows:(c + 1) * rows, :],
                           preferred_element_type=F32)
        y = jnp.clip(acc.astype(BF16), -8.0, 8.0).astype(F32)
        heads = []
        is_kv = lax.rem(j, 4) == 3
        for i in range(heads_per):
            piece = y[:, i * 128:(i + 1) * 128]
            turned = (piece * cos + pltpu.roll(piece, 64, 1) * sin).astype(BF16).astype(F32)
            heads.append(turned if i == 0 else jnp.where(is_kv, piece, turned))
        recv[j] = jnp.concatenate(heads, axis=1)
    with jax.named_scope("barrier"):
        pl.semaphore_wait(barrier, n_sp - 1 + KV)

    def q_start(d, carry):
        pltpu.make_async_remote_copy(
            src_ref=recv.at[j], dst_ref=recv.at[j], send_sem=q_send, recv_sem=q_recv,
            device_id={"sp": base + lax.rem(j + d, PLANE)}, device_id_type=MESH).start()
        return carry

    with jax.named_scope("qsend"):
        lax.fori_loop(1, PLANE, q_start, 0)
    q_others = recv.at[pl.ds(0, PLANE - 1)]
    with jax.named_scope("qwait"):
        pltpu.make_async_copy(q_others, q_others, q_recv).wait()
    with jax.named_scope("spread"):
        for blk in range(PLANE):
            for i in range(heads_per):
                xs[pl.ds(blk * heads_per + i, n_seq, stride=32), :] = recv[blk, :, i * 128:(i + 1) * 128]
        xb[...] = xs[...].astype(BF16)
        new_ref[...] = xb[...]

    row8 = lax.broadcasted_iota(jnp.int32, (32, 128), 0) % 8
    diag = lax.broadcasted_iota(jnp.int32, (32, 128), 1) == row8

    def spread(col_vec, n):
        tiles = jnp.where(diag[:8 * n], col_vec, 0.0).reshape(n, 8, 128)
        return jnp.broadcast_to(jnp.sum(tiles, axis=1, keepdims=True), (n, 8, 128)).reshape(8 * n, 128)

    with jax.named_scope("kvwait"):
        k_copy.wait()
        v_copy.wait()
    row = lax.broadcasted_iota(jnp.int32, (32, n_rows), 0)
    col = lax.broadcasted_iota(jnp.int32, (32, n_rows), 1)
    seq_of = jnp.where(col % KV == row // 8, col // KV + sp * seq_local, 1 << 30)
    scale = 128 ** -0.5
    with jax.named_scope("attn"):
        for i in range(1, n_lines + 1):
            ln = lax.rem(line + i, n_lines)
            for t in range(2):
                b = ln * 2 + t
                q = xb[pl.ds(pl.multiple_of(b * 32, 32), 32), :]
                s = lax.dot_general(q, k_buf[b], (((1,), (1,)), ((), ())), preferred_element_type=F32) * scale
                s = jnp.where(seq_of < pos_ref[b], s, NEG)
                m = jnp.max(s, axis=1, keepdims=True)
                e = jnp.exp(s - m)
                l = jnp.sum(e, axis=1, keepdims=True)
                o = jnp.dot(e.astype(BF16), v_buf[b], preferred_element_type=F32)
                o = jnp.where(row8 == 6, spread(m, KV), jnp.where(row8 == 7, spread(l, KV), o))
                part[ln, :, t] = o.reshape(KV, 8, 128)
            for d in range(KV):
                if i == n_lines and d == 0:
                    continue
                to = lax.rem(group + d, KV)
                pltpu.make_async_remote_copy(
                    src_ref=part.at[ln, to], dst_ref=parts.at[sp], send_sem=rs_send, recv_sem=rs_recv,
                    device_id={"sp": ln * KV + to}, device_id_type=MESH).start()
        parts[sp] = part[line, group]

    with jax.named_scope("newrow"):
        fresh = []
        for t in range(2):
            tile = xs[pl.ds(pl.multiple_of((line * 2 + t) * 32 + group * 8, 8), 8), :]
            score = jnp.sum(tile * tile[6:7, :], axis=1, keepdims=True) * scale
            fresh.append((spread(score, 1)[:1], tile[7:8, :]))

    others = parts.at[pl.ds(0, n_sp - 1)]
    with jax.named_scope("rswait"):
        pltpu.make_async_copy(others, others, rs_recv).wait()
    with jax.named_scope("merge"):
        lane = lax.broadcasted_iota(jnp.int32, (1, 128), 1)
        lhs[...] = jnp.zeros_like(lhs)
        flat = parts.reshape(n_sp * 16, 128)
        for t in range(2):
            m = flat[pl.ds(t * 8 + 6, n_sp, stride=16), :]
            l = flat[pl.ds(t * 8 + 7, n_sp, stride=16), :]
            m_new, v_new = fresh[t]
            top = jnp.maximum(jnp.max(m, axis=0, keepdims=True), m_new)
            f = jnp.exp(m - top)
            f_new = jnp.exp(m_new - top)
            den = jnp.where(lane < 6, jnp.sum(f * l, axis=0, keepdims=True) + f_new, 1.0)
            wt = (jnp.concatenate([f, jnp.broadcast_to(f_new, (8, 128))], axis=0) / den).T
            sums = [wt[:8, n_sp:n_sp + 1] * v_new] + [jnp.zeros((8, 128), F32)] * 3
            for s in range(n_sp):
                sums[s % 4] += wt[:8, s:s + 1] * parts[s, t]
            acc = (sums[0] + sums[1]) + (sums[2] + sums[3])
            for hd in range(6):
                lhs[t:t + 1, hd * 128:(hd + 1) * 128] = acc[hd:hd + 1, :]

    me = group * 2 + tp
    with jax.named_scope("wout"):
        left = lhs[...].astype(BF16)
        for c in range(OWNERS):
            wo_copy(c).wait()
            res = jnp.dot(left, wo_buf[:, c * own:(c + 1) * own], preferred_element_type=F32)
            for t in range(2):
                for cb in range(n_cb):
                    mine[c, t, cb:cb + 1, :] = res[t:t + 1, cb * 128:(cb + 1) * 128]
                mine[c, t, n_cb:8, :] = jnp.zeros((8 - n_cb, 128), F32)

    with jax.named_scope("xsend"):
        for d in range(1, OWNERS):
            owner = lax.rem(me + d, OWNERS)
            pltpu.make_async_remote_copy(
                src_ref=mine.at[owner], dst_ref=shares.at[me], send_sem=x_send, recv_sem=x_recv,
                device_id={"tp": lax.rem(owner, 2), "sp": line * KV + lax.div(owner, 2)}, device_id_type=MESH).start()
        shares[me] = mine[me]
    x_others = shares.at[pl.ds(0, OWNERS - 1)]
    slot = group * n_lines + line
    with jax.named_scope("xwait"):
        pltpu.make_async_copy(x_others, x_others, x_recv).wait()
    with jax.named_scope("agsend"):
        total = shares[0]
        for s in range(1, OWNERS):
            total += shares[s]
        full[slot] = total

        def ag_start(d, carry):
            pltpu.make_async_remote_copy(
                src_ref=full.at[slot], dst_ref=full.at[slot], send_sem=ag_send, recv_sem=ag_recv,
                device_id={"sp": lax.rem(sp + d, n_sp)}, device_id_type=MESH).start()
            return carry

        lax.fori_loop(1, n_sp, ag_start, 0)
    f_others = full.at[pl.ds(0, n_sp - 1)]
    with jax.named_scope("agwait"):
        pltpu.make_async_copy(f_others, f_others, ag_recv).wait()
    swap = pltpu.make_async_remote_copy(
        src_ref=full, dst_ref=other, send_sem=tp_send, recv_sem=tp_recv, device_id={"tp": 1 - tp},
        device_id_type=MESH)
    swap.start()

    def finish(buf, core):
        buf = buf.reshape(n_sp * 16, 128)
        for g in range(KV):
            for cb in range(n_cb):
                slab = buf[pl.ds(g * n_lines * 16 + cb, n_seq, stride=8), :]
                at = pl.ds(pl.multiple_of((g * 2 + core) * own + cb * 128, 128), 128)
                out_ref[:, at] = (h_ref[:, at].astype(F32) + slab).astype(BF16)

    with jax.named_scope("finish1"):
        finish(full, tp)
    with jax.named_scope("swapwait"):
        swap.wait()
    with jax.named_scope("finish2"):
        finish(other, 1 - tp)
    with jax.named_scope("drain"):
        pltpu.make_async_copy(q_others, q_others, q_send).wait()
        pltpu.make_async_copy(others, others, rs_send).wait()
        pltpu.make_async_copy(x_others, x_others, x_send).wait()
        pltpu.make_async_copy(f_others, f_others, ag_send).wait()


def cache_kernel(pos_ref, new_ref, k_ref, v_ref, k_out, v_out, new_k, new_v, sem, row_sem):
    n_seq, seq_local = k_ref.shape[:2]
    base = lax.axis_index("sp") * seq_local
    copies = [pltpu.make_async_copy(k_ref, k_out, sem.at[0]), pltpu.make_async_copy(v_ref, v_out, sem.at[1])]
    for c in copies:
        c.start()
    for b in range(n_seq):
        tile = new_ref[b * 32:(b + 1) * 32, :].astype(F32)
        for buf, r in ((new_k, 6), (new_v, 7)):
            buf[b] = jnp.concatenate([tile[g * 8 + r:g * 8 + r + 1, :] for g in range(KV)], axis=0).astype(BF16)
    for c in copies:
        c.wait()

    def rows(b):
        at = pos_ref[b] - base
        return at, [pltpu.make_async_copy(new_k.at[b], k_out.at[b, at], row_sem),
                    pltpu.make_async_copy(new_v.at[b], v_out.at[b, at], row_sem)]

    for phase in range(2):
        for b in range(n_seq):
            at, pair = rows(b)

            @pl.when(jnp.logical_and(at >= 0, at < seq_local))
            def _():
                for c in pair:
                    if phase == 0:
                        c.start()
                    else:
                        c.wait()


def solution(mesh):
    cache_spec = P('dp', 'sp', 'tp', None)
    n_sp = mesh.shape["sp"]

    def local_step(hidden, norm_scale, w_qkv, w_out, k_cache, v_cache, positions):
        n_seq, seq_local, kv, head_dim = k_cache.shape
        d_model = hidden.shape[1]
        width = w_qkv.shape[1] // PLANE
        depth = w_out.shape[0] // kv
        vmem = pl.BlockSpec(memory_space=VMEM)
        smem = pl.BlockSpec(memory_space=pltpu.SMEM)
        hbm = pl.BlockSpec(memory_space=pltpu.HBM)
        half = head_dim // 2
        freq = np.exp(np.arange(half, dtype=np.float32) * np.float32(-2.0 * math.log(500000.0) / head_dim))
        freq = jnp.asarray(np.concatenate([freq, freq])[None].astype(np.float32))
        flat = (n_seq, seq_local * kv, head_dim)
        dma = pltpu.SemaphoreType.DMA

        h_out, new_rows = pl.pallas_call(
            step_kernel,
            out_shape=[jax.ShapeDtypeStruct((n_seq, d_model), BF16), jax.ShapeDtypeStruct((n_seq * 32, head_dim), BF16)],
            in_specs=[hbm] * 8,
            out_specs=[vmem, vmem],
            scratch_shapes=[
                pltpu.SMEM((n_seq,), jnp.int32),
                VMEM((n_seq, d_model), BF16),
                VMEM((d_model,), BF16),
                VMEM((1, head_dim), F32),
                dma((4,)),
                VMEM((d_model, width), BF16),
                VMEM((depth, d_model), BF16),
                VMEM(flat, BF16),
                VMEM(flat, BF16),
                VMEM((PLANE, n_seq, width), F32),
                VMEM((n_seq * 32, head_dim), F32),
                VMEM((n_seq * 32, head_dim), BF16),
                VMEM((n_seq // 2, kv, 2, 8, head_dim), F32),
                VMEM((n_sp, 2, 8, head_dim), F32),
                VMEM((8, depth), F32),
                VMEM((OWNERS, 2, 8, head_dim), F32),
                VMEM((OWNERS, 2, 8, head_dim), F32),
                VMEM((n_sp, 2, 8, head_dim), F32),
                VMEM((n_sp, 2, 8, head_dim), F32),
                dma((K_CHUNKS,)), dma((OWNERS,)), dma((2,)),
            ] + [dma] * 10,
            compiler_params=pltpu.CompilerParams(
                collective_id=0, has_side_effects=True, vmem_limit_bytes=32 * 1024 * 1024),
            cost_estimate=pl.CostEstimate(flops=60_000_000_000, bytes_accessed=20_000_000, transcendentals=0),
            name="step",
        )(*[pltpu.with_memory_space_constraint(a, pltpu.HBM) for a in (
            positions, hidden, norm_scale, freq, w_qkv, w_out, k_cache.reshape(flat), v_cache.reshape(flat))])

        k_new, v_new = pl.pallas_call(
            cache_kernel,
            out_shape=[jax.ShapeDtypeStruct(k_cache.shape, BF16)] * 2,
            in_specs=[smem, vmem, vmem, vmem],
            out_specs=[hbm, hbm],
            scratch_shapes=[VMEM((n_seq, kv, head_dim), BF16)] * 2 + [dma((2,)), dma],
            compiler_params=pltpu.CompilerParams(vmem_limit_bytes=16 * 1024 * 1024),
            name="cache",
        )(positions, new_rows, pltpu.with_memory_space_constraint(k_cache, VMEM),
          pltpu.with_memory_space_constraint(v_cache, VMEM))
        return h_out, k_new, v_new

    return jax.shard_map(
        local_step,
        mesh=mesh,
        in_specs=(P('dp', None), P(None), P(None, 'tp'), P('tp', None), cache_spec, cache_spec, P('dp')),
        out_specs=(P('dp', None), cache_spec, cache_spec),
        check_vma=False,
    )
```

time: 572 us -> 56.1 us (0.10)
  blocking collectives: 296 us -> 0 us
  waiting for transfers between devices: 202 us -> 0 us
  Pallas kernels: 0 us -> 54.5 us
  matrix products: 38.1 us -> 0 us
  other arithmetic: 15.7 us -> 0 us
  between operations: 14.2 us -> 0.7 us
    pmax x1 -> x0, blocking collectives: 296 us -> none  [local_step(): global_max = lax.pmax(local_max, 'sp')]
    psum x2 -> x0, waiting for transfers between devices: 202 us -> none  [the longest x1 178 us: local_step(): merged = lax.psum(packed, 'sp')]
    pallas_call x0 -> x2, Pallas kernels: none -> 54.5 us  [the longest x1 51.9 us: local_step(): pl.pallas_call(step_kernel, out_shape=[jax.ShapeDtypeStruct((n_seq, d_mod...]
    dot_general x4 -> x0, matrix products: 38.1 us -> none  [the longest x1 20 us: local_step(): jnp.dot(normed, w_qkv, preferred_element_type=jnp.float32)]
    select_n x1 -> x0, other arithmetic: 6.94 us -> none  [local_step(): v_upd = jnp.where(new_row, grouped[:, :, q_per_kv + 1][:, None], v_cache)]
  transfers between devices with their start and end apart: 2 -> 0, of which waited for: 2 -> 0; matrix products, arithmetic and copies ran while one was open for 0% -> 0% of each run, Pallas kernels for 0% -> 0%
where the time goes in v2:
time: 56.1 us; the launch traced here: 56 us
  Pallas kernels  54.5 us (97%)
  local copies, waits for them, and re-layouts  0.76 us (1%)
  between operations  0.7 us (1%)
    pallas_call x1, Pallas kernels, local_step(): pl.pallas_call(step_kernel, out_shape=[jax.ShapeDtypeStruct((n_seq, d_mod...  51.9 us
    pallas_call x1, Pallas kernels, local_step(): pl.pallas_call(cache_kernel, out_shape=[jax.ShapeDtypeStruct(k_cache.shap...  2.58 us

profile of v2, /device:TPU:1, one launch (start us, length us, event | category | flops | bytes accessed | tf_op | source)
XLA Modules:
  0.0 56.0 jit_solution(4237640209294689734)
XLA Ops:
  0.6 0.0 copy-start
  0.6 0.0 copy-start.1
  0.7 0.0 copy-start.2
  0.7 51.9 %step.1 = (bf16[32,6144]{1,0:T(8,128)(2,1)S(1)}, bf16[1024,128]{1,0:T(8,128)(2,1)S(1)}) custom-call(s32[32]{0:T(128)} %pos_ref.1, bf16[32,6144]{1,0:T(8,128)(2,1)} %h_hbm.1, bf16[6144]{0:T(1024)(128)(2,1)} %scale_hbm.1, f32[1,128]{1,0:T(1,128)} %constant.2.clone.freq_hbm, bf16[6144,4096]{1,0:T(8,128)(2,1)} %wq_ref.1, bf16[3072,6144]{1,0:T(8,128)(2,1)} %wo_ref.1, ...), custom_call_target="tpu_custom_call" | custom-call | flops 60000002048 | bytes 20000000 | tf_op jit(solution)/shard_map/step/pallas_call | solution.py:311
  52.6 0.0 copy-done
  52.6 0.0 copy-done.1
  52.6 0.0 copy-done.2
  52.6 2.6 %cache.1 = (bf16[32,64,4,128]{3,2,1,0:T(4,128)(2,1)}, bf16[32,64,4,128]{3,2,1,0:T(4,128)(2,1)}) custom-call(s32[32]{0:T(128)S(1)} %copy-done.2, bf16[1024,128]{1,0:T(8,128)(2,1)S(1)} %get-tuple-element.8.new_ref, bf16[32,64,4,128]{3,2,1,0:T(4,128)(2,1)S(1)} %copy-done, bf16[32,64,4,128]{3,2,1,0:T(4,128)(2,1)S(1)} %copy-done.1), custom_call_target="tpu_custom_call" | custom-call | tf_op jit(solution)/shard_map/cache/pallas_call | solution.py:345
  55.2 0.7 %copy.12 = bf16[32,6144]{1,0:T(8,128)(2,1)} copy(bf16[32,6144]{1,0:T(8,128)(2,1)S(1)} %get-tuple-element.14) | data formatting | bytes 786432
Async XLA Ops:
  0.6 52.0 %copy-start = (bf16[32,64,4,128]{3,2,1,0:T(4,128)(2,1)S(1)}, bf16[32,64,4,128]{3,2,1,0:T(4,128)(2,1)}, u32[]{:S(2)}) copy-start(bf16[32,64,4,128]{3,2,1,0:T(4,128)(2,1)} %k_ref.1) | copy-start | bytes 6291460
  0.6 52.0 %copy-start.1 = (bf16[32,64,4,128]{3,2,1,0:T(4,128)(2,1)S(1)}, bf16[32,64,4,128]{3,2,1,0:T(4,128)(2,1)}, u32[]{:S(2)}) copy-start(bf16[32,64,4,128]{3,2,1,0:T(4,128)(2,1)} %v_ref.1) | copy-start | bytes 6291460
  0.7 52.0 %copy-start.2 = (s32[32]{0:T(128)S(1)}, s32[32]{0:T(128)}, u32[]{:S(2)}) copy-start(s32[32]{0:T(128)} %pos_ref.1) | copy-start | bytes 388

commit v3 on v2

v3 whole, which is shorter than its diff:
```python
import itertools
import math

import jax
import jax.numpy as jnp
import numpy as np
from jax import lax
from jax.experimental import pallas as pl
from jax.experimental.pallas import tpu as pltpu
from jax.sharding import PartitionSpec as P

MESH = pl.DeviceIdType.MESH
VMEM = pltpu.VMEM
F32 = jnp.float32
BF16 = jnp.bfloat16
NEG = -3.0e38
PLANE = 16
K_CHUNKS = 6
KV = 4
OWNERS = 8
CHUNK = 4
RS_ROWS = 14
AG_ROWS = 12


def farthest_first(dims):
    near = lambda o: sum(min(v, 4 - v) for v in o)
    return sorted((o for o in itertools.product(range(4), repeat=dims) if any(o)), key=lambda o: -near(o))


PLANE_ORDER = farthest_first(2)
CUBE_ORDER = farthest_first(3)


def step_kernel(pos_hbm, h_hbm, scale_hbm, freq_hbm, wq_ref, wo_ref, k_ref, v_ref, out_ref, new_ref,
                pos_ref, h_ref, scale_ref, freq_ref, in_sem,
                wq_buf, wo_buf, k_buf, v_buf, recv, xs, xb, part, parts, lhs, mine, shares, full, other,
                wq_sem, wo_sem, kv_sem, q_send, q_recv, early_send, early_recv, late_send, late_recv,
                rs_send, rs_recv, x_send, x_recv, ag_send, ag_recv, tp_send, tp_recv):
    sp = lax.axis_index("sp")
    tp = lax.axis_index("tp")
    n_sp = 64
    line, group = lax.div(sp, KV), lax.rem(sp, KV)
    n_lines = n_sp // KV
    j = lax.rem(sp, PLANE)
    base = sp - j
    y_at, x_at = lax.div(j, 4), lax.rem(j, 4)
    is_kv = x_at == 3
    n_seq, d_model = h_ref.shape
    width = wq_buf.shape[1]
    heads_per = width // 128
    rows = d_model // K_CHUNKS
    n_rows = k_ref.shape[1]
    seq_local = n_rows // KV
    depth = wo_buf.shape[0]
    own = d_model // OWNERS
    n_cb = own // 128

    def wq_copy(c):
        return pltpu.make_async_copy(
            wq_ref.at[pl.ds(c * rows, rows), pl.ds(pl.multiple_of(j * width, width), width)],
            wq_buf.at[pl.ds(c * rows, rows)], wq_sem.at[c])

    wo_copy = pltpu.make_async_copy(wo_ref.at[pl.ds(pl.multiple_of(group * depth, depth), depth)], wo_buf, wo_sem)
    k_copy = pltpu.make_async_copy(k_ref, k_buf, kv_sem.at[0])
    v_copy = pltpu.make_async_copy(v_ref, v_buf, kv_sem.at[1])
    small = [pltpu.make_async_copy(src, dst, in_sem.at[i]) for i, (src, dst) in enumerate(
        [(h_hbm, h_ref), (pos_hbm, pos_ref), (freq_hbm, freq_ref), (scale_hbm, scale_ref)])]
    for c in small:
        c.start()
    for c in range(K_CHUNKS):
        wq_copy(c).start()

    barrier = pltpu.get_barrier_semaphore()

    def greet(d, carry):
        pl.semaphore_signal(barrier, inc=1, device_id={"sp": lax.rem(sp + d, n_sp)}, device_id_type=MESH)
        return carry

    with jax.named_scope("greet"):
        lax.fori_loop(1, n_sp, greet, 0)
        for d in range(KV):
            pl.semaphore_signal(barrier, inc=1, device_id={"tp": 1 - tp, "sp": line * KV + lax.rem(group + d, KV)},
                                device_id_type=MESH)

    with jax.named_scope("hwait"):
        small[0].wait()
    with jax.named_scope("norm"):
        hidden = h_ref[...].astype(F32)
        centered = hidden - jnp.mean(hidden, axis=-1, keepdims=True)
        var = jnp.mean(centered * centered, axis=-1, keepdims=True)
    with jax.named_scope("inwait"):
        for c in small[1:]:
            c.wait()
        k_copy.start()
        v_copy.start()
    with jax.named_scope("norm2"):
        u = (centered * lax.rsqrt(var + 1e-5) * scale_ref[...].astype(F32)[None, :]).astype(BF16)
        seq_row = lax.broadcasted_iota(jnp.int32, (n_seq, 128), 0)
        pos = jnp.zeros((n_seq, 128), jnp.int32)
        for b in range(n_seq):
            pos = jnp.where(seq_row == b, pos_ref[b], pos)
        angles = pos.astype(F32) * freq_ref[...]
        cos = jnp.cos(angles)
        sin = jnp.sin(angles)
        sin = jnp.where(lax.broadcasted_iota(jnp.int32, (n_seq, 128), 1) < 64, -sin, sin)

    with jax.named_scope("qkv"):
        acc = jnp.zeros((n_seq, width), F32)
        for c in range(K_CHUNKS):
            wq_copy(c).wait()
            acc += jnp.dot(u[:, c * rows:(c + 1) * rows], wq_buf[c * rows:(c + 1) * rows, :],
                           preferred_element_type=F32)
        y = jnp.clip(acc.astype(BF16), -8.0, 8.0).astype(F32)
        heads = []
        for i in range(heads_per):
            piece = y[:, i * 128:(i + 1) * 128]
            turned = (piece * cos + pltpu.roll(piece, 64, 1) * sin).astype(BF16).astype(F32)
            heads.append(turned if i == 0 else jnp.where(is_kv, piece, turned))
        recv[j] = jnp.concatenate(heads, axis=1)
        wo_copy.start()
    with jax.named_scope("barrier"):
        pl.semaphore_wait(barrier, n_sp - 1 + KV)

    def to_plane(dy, dx, send_sem, recv_sem):
        peer = base + lax.rem(y_at + dy, 4) * 4 + lax.rem(x_at + dx, 4)
        return pltpu.make_async_remote_copy(
            src_ref=recv.at[j], dst_ref=recv.at[j], send_sem=send_sem, recv_sem=recv_sem,
            device_id={"sp": peer}, device_id_type=MESH)

    def blocks(n):
        return recv.at[pl.ds(0, n)]

    def wait_for(n, sem):
        pltpu.make_async_copy(blocks(n), blocks(n), sem).wait()

    is_last = jnp.logical_and(is_kv, y_at == 3)
    with jax.named_scope("qsend"):
        @pl.when(jnp.logical_not(is_kv))
        def _():
            for dy, dx in PLANE_ORDER:
                to_plane(dy, dx, q_send, q_recv).start()

        @pl.when(is_kv)
        def _():
            for dy in (2, 1, 3, 0):
                @pl.when(jnp.logical_or(dy != 0, y_at != 3))
                def _():
                    to_plane(dy, lax.rem(y_at + 1, 4), early_send, early_recv).start()

        for g in range(KV):
            for r in (6, 7):
                xs[pl.ds(g * 8 + r, n_seq, stride=32), :] = jnp.zeros((n_seq, 128), F32)
    with jax.named_scope("qwait"):
        @pl.when(is_kv)
        def _():
            wait_for(12, q_recv)

        @pl.when(jnp.logical_not(is_kv))
        def _():
            wait_for(11, q_recv)
    with jax.named_scope("spread"):
        for blk in range(PLANE):
            if blk % 4 == 3:
                continue
            for i in range(heads_per):
                xs[pl.ds(blk * heads_per + i, n_seq, stride=32), :] = recv[blk, :, i * 128:(i + 1) * 128]
        xb[...] = xs[...].astype(BF16)

    row8 = lax.broadcasted_iota(jnp.int32, (32, 128), 0) % 8
    lane32 = lax.broadcasted_iota(jnp.int32, (32, 128), 1)

    def as_rows(cols, n):
        tiles = sum(jnp.where((lane32 == row8 + 8 * t)[:8 * n], c, 0.0) for t, c in enumerate(cols)).reshape(n, 8, 128)
        return jnp.broadcast_to(jnp.sum(tiles, axis=1, keepdims=True), (n, 8, 128)).reshape(8 * n, 128)

    with jax.named_scope("kvwait"):
        k_copy.wait()
        v_copy.wait()
    row = lax.broadcasted_iota(jnp.int32, (32, n_rows), 0)
    col = lax.broadcasted_iota(jnp.int32, (32, n_rows), 1)
    seq_of = jnp.where(col % KV == row // 8, col // KV + sp * seq_local, 1 << 30)
    scale = 128 ** -0.5

    def line_at(i):
        return lax.rem(line + 1 + i, n_lines)

    def scores(c):
        out = []
        for i in range(CHUNK):
            for t in range(2):
                b = line_at(c * CHUNK + i) + 16 * t
                q = xb[pl.ds(pl.multiple_of(b * 32, 32), 32), :]
                s = lax.dot_general(q, k_buf[b], (((1,), (1,)), ((), ())), preferred_element_type=F32) * scale
                out.append(jnp.where(seq_of < pos_ref[b], s, NEG))
        return out

    with jax.named_scope("attn"):
        n_chunks = n_lines // CHUNK
        held = scores(0)
        for c in range(n_chunks):
            ahead = scores(c + 1) if c + 1 < n_chunks else None
            for i in range(CHUNK):
                ln = line_at(c * CHUNK + i)
                stats, outs = [], []
                for t in range(2):
                    s = held[i * 2 + t]
                    m = jnp.max(s, axis=1, keepdims=True)
                    e = jnp.exp(s - m)
                    stats.append((m, jnp.sum(e, axis=1, keepdims=True)))
                    outs.append(jnp.dot(e.astype(BF16), v_buf[ln + 16 * t], preferred_element_type=F32))
                (m0, l0), (m1, l1) = stats
                first = jnp.where(row8 == 6, as_rows((m0, m1), KV), jnp.where(row8 == 7, as_rows((l0, l1), KV), outs[0]))
                for g in range(KV):
                    at = pl.multiple_of((ln * KV + g) * 16, 16)
                    part[pl.ds(at, 8), :] = first[g * 8:(g + 1) * 8]
                    part[pl.ds(at + 8, 8), :] = outs[1][g * 8:(g + 1) * 8]
            for i in range(CHUNK):
                ln = line_at(c * CHUNK + i)
                for d in (2, 1, 3, 0):
                    if c * CHUNK + i == n_lines - 1 and d == 0:
                        continue
                    to = lax.rem(group + d, KV)
                    pltpu.make_async_remote_copy(
                        src_ref=part.at[pl.ds(pl.multiple_of((ln * KV + to) * 16, 16), RS_ROWS)],
                        dst_ref=parts.at[pl.ds(pl.multiple_of(sp * 16, 16), RS_ROWS)], send_sem=rs_send,
                        recv_sem=rs_recv, device_id={"sp": ln * KV + to}, device_id_type=MESH).start()
            held = ahead
        parts[pl.ds(pl.multiple_of(sp * 16, 16), 16), :] = part[pl.ds(pl.multiple_of(sp * 16, 16), 16), :]

    with jax.named_scope("newrow"):
        @pl.when(jnp.logical_not(is_last))
        def _():
            wait_for(1, early_recv)

        for i in range(heads_per):
            xs[pl.ds(group * 8 + 6 + i, n_seq, stride=32), :] = recv[group * 4 + 3, :, i * 128:(i + 1) * 128]
        cols, v_new = [], []
        for t in range(2):
            tile = xs[pl.ds(pl.multiple_of((line + 16 * t) * 32 + group * 8, 8), 8), :]
            cols.append(jnp.sum(tile * tile[6:7, :], axis=1, keepdims=True) * scale)
            v_new.append(tile[7:8, :])
        m_new = as_rows(cols, 1)[:1]

    rs_others = parts.at[pl.ds(0, (n_sp - 1) * RS_ROWS)]
    with jax.named_scope("rswait"):
        pltpu.make_async_copy(rs_others, rs_others, rs_recv).wait()

    with jax.named_scope("latesend"):
        @pl.when(is_kv)
        def _():
            for dx in (1, 2, 3, 4):
                for dy in (0, 1, 2, 3):
                    to_x = lax.rem(x_at + dx, 4)
                    ok = to_x != y_at
                    if dx == 4 and dy == 0:
                        continue

                    @pl.when(ok)
                    def _():
                        to_plane(dy, dx, late_send, late_recv).start()

    with jax.named_scope("merge"):
        lane = lax.broadcasted_iota(jnp.int32, (1, 128), 1)
        m = parts[pl.ds(6, n_sp, stride=16), :]
        l = parts[pl.ds(7, n_sp, stride=16), :]
        top = jnp.maximum(jnp.max(m, axis=0, keepdims=True), m_new)
        f = jnp.exp(m - top)
        f_new = jnp.exp(m_new - top)
        real = jnp.logical_and(lane < 16, lane % 8 < 6)
        den = jnp.where(real, jnp.sum(f * l, axis=0, keepdims=True) + f_new, 1.0)
        wt = (jnp.concatenate([f, jnp.broadcast_to(f_new, (8, 128))], axis=0) / den).T
        lhs[...] = jnp.zeros_like(lhs)
        for t in range(2):
            w8 = wt[t * 8:(t + 1) * 8]
            sums = [w8[:, n_sp:n_sp + 1] * v_new[t]] + [jnp.zeros((8, 128), F32)] * 3
            for s in range(n_sp):
                sums[s % 4] += w8[:, s:s + 1] * parts[s * 16 + t * 8:s * 16 + t * 8 + 8, :]
            acc = (sums[0] + sums[1]) + (sums[2] + sums[3])
            for hd in range(6):
                lhs[t:t + 1, hd * 128:(hd + 1) * 128] = acc[hd:hd + 1, :]

    me = group * 2 + tp
    with jax.named_scope("wowait"):
        wo_copy.wait()
    with jax.named_scope("wout"):
        left = lhs[...].astype(BF16)
        order = [(dg, dt) for dg in (2, 1, 3, 0) for dt in (1, 0)]

        def product(k):
            owner = lax.rem(group + order[k][0], KV) * 2 + (tp if order[k][1] == 0 else 1 - tp)
            at = pl.multiple_of(owner * own, own)
            return owner, jnp.dot(left, wo_buf[:, pl.ds(at, own)], preferred_element_type=F32)

        held = product(0)
        for k in range(OWNERS):
            ahead = product(k + 1) if k + 1 < OWNERS else None
            owner, res = held
            buf = mine if k < OWNERS - 1 else shares
            at = pl.multiple_of(owner * 16, 16)
            for t in range(2):
                for cb in range(n_cb):
                    buf[pl.ds(at + t * n_cb + cb, 1), :] = res[t:t + 1, cb * 128:(cb + 1) * 128]
            if k < OWNERS - 1:
                pltpu.make_async_remote_copy(
                    src_ref=mine.at[pl.ds(at, AG_ROWS)],
                    dst_ref=shares.at[pl.ds(pl.multiple_of(me * 16, 16), AG_ROWS)], send_sem=x_send, recv_sem=x_recv,
                    device_id={"tp": lax.rem(owner, 2), "sp": line * KV + lax.div(owner, 2)},
                    device_id_type=MESH).start()
            held = ahead

    x_others = shares.at[pl.ds(0, (OWNERS - 1) * AG_ROWS)]
    slot = group * n_lines + line
    with jax.named_scope("xwait"):
        pltpu.make_async_copy(x_others, x_others, x_recv).wait()
    z_at = lax.div(sp, PLANE)
    with jax.named_scope("agsend"):
        total = shares[0:16, :]
        for s in range(1, OWNERS):
            total += shares[s * 16:(s + 1) * 16, :]
        at = pl.multiple_of(slot * 16, 16)
        full[pl.ds(at, 16), :] = total
        zs = [lax.rem(z_at + d, 4) * 16 for d in range(4)]
        ys = [lax.rem(y_at + d, 4) * 4 for d in range(4)]
        xs_ = [lax.rem(x_at + d, 4) for d in range(4)]
        for dz, dy, dx in CUBE_ORDER:
            pltpu.make_async_remote_copy(
                src_ref=full.at[pl.ds(at, AG_ROWS)], dst_ref=full.at[pl.ds(at, AG_ROWS)], send_sem=ag_send,
                recv_sem=ag_recv.at[group], device_id={"sp": zs[dz] + ys[dy] + xs_[dx]}, device_id_type=MESH).start()

    def finish(buf, g, core):
        for cb in range(n_cb):
            at = pl.ds(pl.multiple_of((g * 2 + core) * own + cb * 128, 128), 128)
            for t in range(2):
                slab = buf[pl.ds(g * n_lines * 16 + t * n_cb + cb, n_lines, stride=16), :]
                out_ref[t * 16:(t + 1) * 16, at] = (h_ref[t * 16:(t + 1) * 16, at].astype(F32) + slab).astype(BF16)

    def quarter(k):
        g = lax.rem(group + k, KV)
        at = pl.ds(pl.multiple_of(g * n_lines * 16, 256), n_lines * 16)
        return g, pltpu.make_async_remote_copy(
            src_ref=full.at[at], dst_ref=other.at[at], send_sem=tp_send.at[k], recv_sem=tp_recv.at[g],
            device_id={"tp": 1 - tp}, device_id_type=MESH)

    with jax.named_scope("agwait"):
        for k in (0, 1, 3, 2):
            g, swap = quarter(k)
            n = (n_lines if k else n_lines - 1) * AG_ROWS
            pltpu.make_async_copy(full.at[pl.ds(0, n)], full.at[pl.ds(0, n)], ag_recv.at[g]).wait()
            swap.start()
            finish(full, g, tp)
    with jax.named_scope("swapwait"):
        for k in (0, 1, 3, 2):
            g, swap = quarter(k)
            swap.wait()
            finish(other, g, 1 - tp)
    with jax.named_scope("drain"):
        @pl.when(jnp.logical_and(is_kv, jnp.logical_not(is_last)))
        def _():
            wait_for(2, late_recv)
            wait_for(4, early_send)
            wait_for(11, late_send)

        @pl.when(is_last)
        def _():
            wait_for(3, late_recv)
            wait_for(3, early_send)
            wait_for(12, late_send)

        @pl.when(jnp.logical_not(is_kv))
        def _():
            wait_for(3, late_recv)
            wait_for(PLANE - 1, q_send)

        for g in range(KV):
            for i in range(heads_per):
                at = (i * KV + g) * n_seq
                new_ref[at:at + n_seq, :] = recv[g * 4 + 3, :, i * 128:(i + 1) * 128]
        pltpu.make_async_copy(rs_others, rs_others, rs_send).wait()
        pltpu.make_async_copy(x_others, x_others, x_send).wait()
        f_others = full.at[pl.ds(0, (n_sp - 1) * AG_ROWS)]
        pltpu.make_async_copy(f_others, f_others, ag_send).wait()


def cache_kernel(pos_ref, new_ref, k_ref, v_ref, h_ref, k_out, v_out, h_out, k_fix, v_fix, sem):
    n_seq, seq_local = k_ref.shape[:2]
    base = lax.axis_index("sp") * seq_local
    trio = ((k_ref, k_fix, k_out), (v_ref, v_fix, v_out))
    hidden = pltpu.make_async_copy(h_ref, h_out, sem.at[2])
    hidden.start()
    for b in range(n_seq):
        at = pos_ref[b] - base
        here = jnp.logical_and(at >= 0, at < seq_local)

        @pl.when(jnp.logical_not(here))
        def _():
            for i, (src, _, dst) in enumerate(trio):
                pltpu.make_async_copy(src.at[b], dst.at[b], sem.at[i]).start()

        @pl.when(here)
        def _():
            for i, (src, fix, dst) in enumerate(trio):
                fix[b] = src[b]
                fix[b, at] = new_ref[pl.ds(i * KV * n_seq + b, KV, stride=n_seq), :].astype(BF16)
                pltpu.make_async_copy(fix.at[b], dst.at[b], sem.at[i]).start()

    for i, (src, _, dst) in enumerate(trio):
        pltpu.make_async_copy(src, dst, sem.at[i]).wait()
    hidden.wait()


def solution(mesh):
    cache_spec = P('dp', 'sp', 'tp', None)
    n_sp = mesh.shape["sp"]

    def local_step(hidden, norm_scale, w_qkv, w_out, k_cache, v_cache, positions):
        n_seq, seq_local, kv, head_dim = k_cache.shape
        d_model = hidden.shape[1]
        width = w_qkv.shape[1] // PLANE
        depth = w_out.shape[0] // kv
        vmem = pl.BlockSpec(memory_space=VMEM)
        smem = pl.BlockSpec(memory_space=pltpu.SMEM)
        hbm = pl.BlockSpec(memory_space=pltpu.HBM)
        half = head_dim // 2
        freq = np.exp(np.arange(half, dtype=np.float32) * np.float32(-2.0 * math.log(500000.0) / head_dim))
        freq = jnp.asarray(np.concatenate([freq, freq])[None].astype(np.float32))
        flat = (n_seq, seq_local * kv, head_dim)
        dma = pltpu.SemaphoreType.DMA

        h_new, new_rows = pl.pallas_call(
            step_kernel,
            out_shape=[jax.ShapeDtypeStruct((n_seq, d_model), BF16), jax.ShapeDtypeStruct((2 * kv * n_seq, head_dim), F32)],
            in_specs=[hbm] * 8,
            out_specs=[vmem, vmem],
            scratch_shapes=[
                pltpu.SMEM((n_seq,), jnp.int32),
                VMEM((n_seq, d_model), BF16),
                VMEM((d_model,), BF16),
                VMEM((1, head_dim), F32),
                dma((4,)),
                VMEM((d_model, width), BF16),
                VMEM((depth, d_model), BF16),
                VMEM(flat, BF16),
                VMEM(flat, BF16),
                VMEM((PLANE, n_seq, width), F32),
                VMEM((n_seq * 32, head_dim), F32),
                VMEM((n_seq * 32, head_dim), BF16),
                VMEM((n_sp * 16, head_dim), F32),
                VMEM((n_sp * 16, head_dim), F32),
                VMEM((8, depth), F32),
                VMEM((OWNERS * 16, head_dim), F32),
                VMEM((OWNERS * 16, head_dim), F32),
                VMEM((n_sp * 16, head_dim), F32),
                VMEM((n_sp * 16, head_dim), F32),
                dma((K_CHUNKS,)), dma, dma((2,)),
            ] + [dma] * 11 + [dma((kv,))] * 3,
            compiler_params=pltpu.CompilerParams(
                collective_id=0, has_side_effects=True, vmem_limit_bytes=32 * 1024 * 1024),
            cost_estimate=pl.CostEstimate(flops=60_000_000_000, bytes_accessed=20_000_000, transcendentals=0),
            name="step",
        )(*[pltpu.with_memory_space_constraint(a, pltpu.HBM) for a in (
            positions, hidden, norm_scale, freq, w_qkv, w_out, k_cache.reshape(flat), v_cache.reshape(flat))])

        k_new, v_new, h_out = pl.pallas_call(
            cache_kernel,
            out_shape=[jax.ShapeDtypeStruct(k_cache.shape, BF16)] * 2 + [jax.ShapeDtypeStruct((n_seq, d_model), BF16)],
            in_specs=[smem, vmem, vmem, vmem, vmem],
            out_specs=[hbm, hbm, hbm],
            scratch_shapes=[VMEM(k_cache.shape, BF16)] * 2 + [dma((3,))],
            compiler_params=pltpu.CompilerParams(vmem_limit_bytes=16 * 1024 * 1024),
            name="cache",
        )(positions, new_rows, pltpu.with_memory_space_constraint(k_cache, VMEM),
          pltpu.with_memory_space_constraint(v_cache, VMEM), h_new)
        return h_out, k_new, v_new

    return jax.shard_map(
        local_step,
        mesh=mesh,
        in_specs=(P('dp', None), P(None), P(None, 'tp'), P('tp', None), cache_spec, cache_spec, P('dp')),
        out_specs=(P('dp', None), cache_spec, cache_spec),
        check_vma=False,
    )
```

time: 56.1 us -> 48.2 us (0.86)
  Pallas kernels: 54.5 us -> 47.4 us
  local copies, waits for them, and re-layouts: 0.76 us -> 0.01 us
    pallas_call x1, Pallas kernels: 51.9 us -> 44.7 us  [local_step(): pl.pallas_call(step_kernel, out_shape=[jax.ShapeDtypeStruct((n_seq, d_mod...]
    unnamed x7 -> x6, local copies, waits for them, and re-layouts: 0.76 us -> 0.01 us
where the time goes in v3:
time: 48.2 us; the launch traced here: 48.1 us
  Pallas kernels  47.4 us (98%)
  between operations  0.69 us (1%)
    pallas_call x1, Pallas kernels, local_step(): pl.pallas_call(step_kernel, out_shape=[jax.ShapeDtypeStruct((n_seq, d_mod...  44.7 us
    pallas_call x1, Pallas kernels, local_step(): pl.pallas_call(cache_kernel, out_shape=[jax.ShapeDtypeStruct(k_cache.shap...  2.65 us

profile of v3, /device:TPU:1, one launch (start us, length us, event | category | flops | bytes accessed | tf_op | source)
XLA Modules:
  0.0 48.1 jit_solution(4476648472423310812)
XLA Ops:
  0.6 0.0 copy-start
  0.6 0.0 copy-start.1
  0.7 0.0 copy-start.2
  0.7 44.7 %step.1 = (bf16[32,6144]{1,0:T(8,128)(2,1)S(1)}, f32[256,128]{1,0:T(8,128)S(1)}) custom-call(s32[32]{0:T(128)} %pos_ref.1, bf16[32,6144]{1,0:T(8,128)(2,1)} %h_hbm.1, bf16[6144]{0:T(1024)(128)(2,1)} %scale_hbm.1, f32[1,128]{1,0:T(1,128)} %constant.2.clone.freq_hbm, bf16[6144,4096]{1,0:T(8,128)(2,1)} %wq_ref.1, bf16[3072,6144]{1,0:T(8,128)(2,1)} %wo_ref.1, ...), custom_call_target="tpu_custom_call" | custom-call | flops 60000002048 | bytes 20000000 | tf_op jit(solution)/shard_map/step/pallas_call | solution.py:430
  45.4 0.0 copy-done
  45.4 0.0 copy-done.1
  45.4 0.0 copy-done.2
  45.4 2.6 %cache.1 = (bf16[32,64,4,128]{3,2,1,0:T(4,128)(2,1)}, bf16[32,64,4,128]{3,2,1,0:T(4,128)(2,1)}, bf16[32,6144]{1,0:T(8,128)(2,1)}) custom-call(s32[32]{0:T(128)S(1)} %copy-done.2, f32[256,128]{1,0:T(8,128)S(1)} %get-tuple-element.8.new_ref, bf16[32,64,4,128]{3,2,1,0:T(4,128)(2,1)S(1)} %copy-done, bf16[32,64,4,128]{3,2,1,0:T(4,128)(2,1)S(1)} %copy-done.1, ...), custom_call_target="tpu_custom_call" | custom-call | tf_op jit(solution)/shard_map/cache/pallas_call | solution.py:464
Async XLA Ops:
  0.6 44.8 %copy-start = (bf16[32,64,4,128]{3,2,1,0:T(4,128)(2,1)S(1)}, bf16[32,64,4,128]{3,2,1,0:T(4,128)(2,1)}, u32[]{:S(2)}) copy-start(bf16[32,64,4,128]{3,2,1,0:T(4,128)(2,1)} %k_ref.1) | copy-start | bytes 6291460
  0.6 44.8 %copy-start.1 = (bf16[32,64,4,128]{3,2,1,0:T(4,128)(2,1)S(1)}, bf16[32,64,4,128]{3,2,1,0:T(4,128)(2,1)}, u32[]{:S(2)}) copy-start(bf16[32,64,4,128]{3,2,1,0:T(4,128)(2,1)} %v_ref.1) | copy-start | bytes 6291460
  0.7 44.8 %copy-start.2 = (s32[32]{0:T(128)S(1)}, s32[32]{0:T(128)}, u32[]{:S(2)}) copy-start(s32[32]{0:T(128)} %pos_ref.1) | copy-start | bytes 388

commit v4 on v3

v4 whole, which is shorter than its diff:
```python
import itertools
import math

import jax
import jax.numpy as jnp
import numpy as np
from jax import lax
from jax.experimental import pallas as pl
from jax.experimental.pallas import tpu as pltpu
from jax.sharding import PartitionSpec as P

MESH = pl.DeviceIdType.MESH
VMEM = pltpu.VMEM
F32 = jnp.float32
BF16 = jnp.bfloat16
NEG = -3.0e38
PLANE = 16
K_CHUNKS = 6
KV = 4
OWNERS = 8
TURNS = (2, 1, 3, 0)
QUARTERS = (0, 1, 3, 2)
RS_ROWS = 14
AG_ROWS = 12


def farthest_first(dims):
    near = lambda o: sum(min(v, 4 - v) for v in o)
    return sorted((o for o in itertools.product(range(4), repeat=dims) if any(o)), key=lambda o: -near(o))


PLANE_ORDER = farthest_first(2)
CUBE_ORDER = farthest_first(3)


def step_kernel(pos_hbm, h_hbm, scale_hbm, freq_hbm, wq_ref, wo_ref, k_ref, v_ref, out_ref, new_ref,
                pos_ref, h_ref, scale_ref, freq_ref, in_sem,
                wq_buf, wo_buf, k_buf, v_buf, recv, xs, xb, part, parts, full, prods, other,
                wq_sem, wo_sem, kv_sem, q_send, q_recv, early_send, early_recv, late_send, late_recv,
                rs_send, rs_recv, ag_send, ag_recv, tp_send, tp_recv, ready):
    sp = lax.axis_index("sp")
    tp = lax.axis_index("tp")
    n_sp = 64
    line, group = lax.div(sp, KV), lax.rem(sp, KV)
    n_lines = n_sp // KV
    j = lax.rem(sp, PLANE)
    base = sp - j
    y_at, x_at = lax.div(j, 4), lax.rem(j, 4)
    z_at = lax.div(sp, PLANE)
    is_kv = x_at == 3
    n_seq, d_model = h_ref.shape
    width = wq_buf.shape[1]
    heads_per = width // 128
    rows = d_model // K_CHUNKS
    n_rows = k_ref.shape[1]
    seq_local = n_rows // KV
    depth = wo_buf.shape[1]
    own = d_model // OWNERS

    def turn_of(dz):
        return jnp.where(dz == 2, 0, jnp.where(dz == 1, 1, jnp.where(dz == 3, 2, 3)))

    def wq_copy(c):
        return pltpu.make_async_copy(
            wq_ref.at[pl.ds(c * rows, rows), pl.ds(pl.multiple_of(j * width, width), width)],
            wq_buf.at[pl.ds(c * rows, rows)], wq_sem.at[c])

    def wo_copy(k):
        g = lax.rem(group + 4 - QUARTERS[k], KV)
        return pltpu.make_async_copy(wo_ref.at[pl.ds(pl.multiple_of(g * depth, depth), depth)], wo_buf.at[g], wo_sem.at[k])

    k_copy = pltpu.make_async_copy(k_ref, k_buf, kv_sem.at[0])
    v_copy = pltpu.make_async_copy(v_ref, v_buf, kv_sem.at[1])
    small = [pltpu.make_async_copy(src, dst, in_sem.at[i]) for i, (src, dst) in enumerate(
        [(h_hbm, h_ref), (pos_hbm, pos_ref), (freq_hbm, freq_ref), (scale_hbm, scale_ref)])]
    for c in small:
        c.start()
    for c in range(K_CHUNKS):
        wq_copy(c).start()

    barrier = pltpu.get_barrier_semaphore()

    with jax.named_scope("greet"):
        for dy, dx in PLANE_ORDER:
            peer = base + lax.rem(y_at + dy, 4) * 4 + lax.rem(x_at + dx, 4)
            pl.semaphore_signal(barrier, inc=1, device_id={"sp": peer}, device_id_type=MESH)
        for dz in range(1, 4):
            pl.semaphore_signal(barrier, inc=1, device_id={"sp": lax.rem(sp + dz * PLANE, n_sp)}, device_id_type=MESH)
        pl.semaphore_signal(barrier, inc=1, device_id={"tp": 1 - tp}, device_id_type=MESH)

    with jax.named_scope("hwait"):
        small[0].wait()
    with jax.named_scope("norm"):
        hidden = h_ref[...].astype(F32)
        centered = hidden - jnp.mean(hidden, axis=-1, keepdims=True)
        var = jnp.mean(centered * centered, axis=-1, keepdims=True)
    with jax.named_scope("inwait"):
        for c in small[1:]:
            c.wait()
        k_copy.start()
        v_copy.start()
    with jax.named_scope("norm2"):
        u = (centered * lax.rsqrt(var + 1e-5) * scale_ref[...].astype(F32)[None, :]).astype(BF16)
        seq_row = lax.broadcasted_iota(jnp.int32, (n_seq, 128), 0)
        pos = jnp.zeros((n_seq, 128), jnp.int32)
        for b in range(n_seq):
            pos = jnp.where(seq_row == b, pos_ref[b], pos)
        angles = pos.astype(F32) * freq_ref[...]
        cos = jnp.cos(angles)
        sin = jnp.sin(angles)
        sin = jnp.where(lax.broadcasted_iota(jnp.int32, (n_seq, 128), 1) < 64, -sin, sin)

    with jax.named_scope("qkv"):
        acc = jnp.zeros((n_seq, width), F32)
        for c in range(K_CHUNKS):
            wq_copy(c).wait()
            acc += jnp.dot(u[:, c * rows:(c + 1) * rows], wq_buf[c * rows:(c + 1) * rows, :],
                           preferred_element_type=F32)
        y = jnp.clip(acc.astype(BF16), -8.0, 8.0).astype(F32)
        heads = []
        for i in range(heads_per):
            piece = y[:, i * 128:(i + 1) * 128]
            turned = (piece * cos + pltpu.roll(piece, 64, 1) * sin).astype(BF16).astype(F32)
            heads.append(turned if i == 0 else jnp.where(is_kv, piece, turned))
        y = jnp.concatenate(heads, axis=1)
        for z in range(4):
            tile = jnp.concatenate([y[z * 4:z * 4 + 4], y[16 + z * 4:16 + z * 4 + 4]], axis=0)
            recv[j, turn_of(lax.rem(z + 4 - z_at, 4))] = tile
        for k in range(KV):
            wo_copy(k).start()
    with jax.named_scope("barrier"):
        pl.semaphore_wait(barrier, PLANE - 1 + 3 + 1)

    def to_plane(dy, dx, send_sem, recv_sem, tiles=pl.ds(0, 4)):
        peer = base + lax.rem(y_at + dy, 4) * 4 + lax.rem(x_at + dx, 4)
        return pltpu.make_async_remote_copy(
            src_ref=recv.at[j, tiles], dst_ref=recv.at[j, tiles], send_sem=send_sem, recv_sem=recv_sem,
            device_id={"sp": peer}, device_id_type=MESH)

    def blocks(n):
        return recv.at[pl.ds(0, n)]

    def wait_for(n, sem):
        pltpu.make_async_copy(blocks(n), blocks(n), sem).wait()

    def wait_for_halves(n, sem):
        flat_half = xs.at[pl.ds(0, n * n_seq * width // 256)]
        pltpu.make_async_copy(flat_half, flat_half, sem).wait()

    is_last = jnp.logical_and(is_kv, y_at == 3)
    with jax.named_scope("qsend"):
        @pl.when(jnp.logical_not(is_kv))
        def _():
            for half in range(2):
                for dy, dx in PLANE_ORDER:
                    to_plane(dy, dx, q_send, q_recv.at[half], pl.ds(half * 2, 2)).start()

        @pl.when(is_kv)
        def _():
            for dy in (2, 1, 3, 0):
                @pl.when(jnp.logical_or(dy != 0, y_at != 3))
                def _():
                    to_plane(dy, lax.rem(y_at + 1, 4), early_send, early_recv).start()

        for dz in range(1, 4):
            pl.semaphore_signal(ready, inc=1, device_id={"sp": lax.rem(sp + dz * PLANE, n_sp)}, device_id_type=MESH)
        for g in range(KV):
            for r in (6, 7):
                xs[pl.ds(g * 8 + r, n_seq, stride=32), :] = jnp.zeros((n_seq, 128), F32)

    def half_queries(half):
        with jax.named_scope(f"qwait{half}"):
            @pl.when(is_kv)
            def _():
                wait_for_halves(12, q_recv.at[half])

            @pl.when(jnp.logical_not(is_kv))
            def _():
                wait_for_halves(11, q_recv.at[half])
        with jax.named_scope("spread"):
            for turn in (half * 2, half * 2 + 1):
                for blk in range(PLANE):
                    if blk % 4 == 3:
                        continue
                    for i in range(heads_per):
                        xs[pl.ds(turn * 256 + blk * heads_per + i, 8, stride=32), :] = (
                            recv[blk, turn, :, i * 128:(i + 1) * 128])
                xb[turn * 256:(turn + 1) * 256, :] = xs[turn * 256:(turn + 1) * 256, :].astype(BF16)

    row8 = lax.broadcasted_iota(jnp.int32, (32, 128), 0) % 8
    lane32 = lax.broadcasted_iota(jnp.int32, (32, 128), 1)

    def as_rows(cols, n):
        tiles = sum(jnp.where((lane32 == row8 + 8 * t)[:8 * n], c, 0.0) for t, c in enumerate(cols)).reshape(n, 8, 128)
        return jnp.broadcast_to(jnp.sum(tiles, axis=1, keepdims=True), (n, 8, 128)).reshape(8 * n, 128)

    with jax.named_scope("kvwait"):
        k_copy.wait()
        v_copy.wait()
    row = lax.broadcasted_iota(jnp.int32, (32, n_rows), 0)
    col = lax.broadcasted_iota(jnp.int32, (32, n_rows), 1)
    seq_of = jnp.where(col % KV == row // 8, col // KV + sp * seq_local, 1 << 30)
    scale = 128 ** -0.5

    def line_at(turn, i):
        return lax.rem(z_at + TURNS[turn], 4) * 4 + lax.rem(y_at + TURNS[i], 4)

    def scores(turn):
        out = []
        for i in range(4):
            for t in range(2):
                at = (turn * 8 + t * 4 + lax.rem(y_at + TURNS[i], 4)) * 32
                b = line_at(turn, i) + 16 * t
                q = xb[pl.ds(pl.multiple_of(at, 32), 32), :]
                s = lax.dot_general(q, k_buf[b], (((1,), (1,)), ((), ())), preferred_element_type=F32) * scale
                out.append(jnp.where(seq_of < pos_ref[b], s, NEG))
        return out

    def values(turn, held):
        for i in range(4):
            ln = line_at(turn, i)
            stats, outs = [], []
            for t in range(2):
                s = held[i * 2 + t]
                m = jnp.max(s, axis=1, keepdims=True)
                e = jnp.exp(s - m)
                stats.append((m, jnp.sum(e, axis=1, keepdims=True)))
                outs.append(jnp.dot(e.astype(BF16), v_buf[ln + 16 * t], preferred_element_type=F32))
            (m0, l0), (m1, l1) = stats
            first = jnp.where(row8 == 6, as_rows((m0, m1), KV), jnp.where(row8 == 7, as_rows((l0, l1), KV), outs[0]))
            for g in range(KV):
                at = pl.multiple_of((ln * KV + g) * 16, 16)
                part[pl.ds(at, 8), :] = first[g * 8:(g + 1) * 8]
                part[pl.ds(at + 8, 8), :] = outs[1][g * 8:(g + 1) * 8]

    def send_partials(turn):
        for i in range(4):
            ln = line_at(turn, i)
            for d in TURNS:
                if turn == 3 and i == 3 and d == 0:
                    continue
                to = lax.rem(group + d, KV)
                pltpu.make_async_remote_copy(
                    src_ref=part.at[pl.ds(pl.multiple_of((ln * KV + to) * 16, 16), RS_ROWS)],
                    dst_ref=parts.at[pl.ds(pl.multiple_of(sp * 16, 16), RS_ROWS)], send_sem=rs_send,
                    recv_sem=rs_recv, device_id={"sp": ln * KV + to}, device_id_type=MESH).start()

    half_queries(0)
    with jax.named_scope("ready"):
        pl.semaphore_wait(ready, 3)
    with jax.named_scope("attn0"):
        held = scores(0)
        ahead = scores(1)
        values(0, held)
        send_partials(0)
        values(1, ahead)
        send_partials(1)
    half_queries(1)
    with jax.named_scope("attn1"):
        held = scores(2)
        ahead = scores(3)
        values(2, held)
        send_partials(2)
        values(3, ahead)
        send_partials(3)
        parts[pl.ds(pl.multiple_of(sp * 16, 16), 16), :] = part[pl.ds(pl.multiple_of(sp * 16, 16), 16), :]

    with jax.named_scope("newrow"):
        @pl.when(jnp.logical_not(is_last))
        def _():
            wait_for(1, early_recv)

        for i in range(heads_per):
            xs[pl.ds(3 * 256 + group * 8 + 6 + i, 8, stride=32), :] = recv[group * 4 + 3, 3, :, i * 128:(i + 1) * 128]
        cols, v_new = [], []
        for t in range(2):
            tile = xs[pl.ds(pl.multiple_of((24 + t * 4 + y_at) * 32 + group * 8, 8), 8), :]
            cols.append(jnp.sum(tile * tile[6:7, :], axis=1, keepdims=True) * scale)
            v_new.append(tile[7:8, :])
        m_new = as_rows(cols, 1)[:1]

    rs_others = parts.at[pl.ds(0, (n_sp - 1) * RS_ROWS)]
    with jax.named_scope("rswait"):
        pltpu.make_async_copy(rs_others, rs_others, rs_recv).wait()

    with jax.named_scope("latesend"):
        @pl.when(is_kv)
        def _():
            for dx in (1, 2, 3, 4):
                for dy in (0, 1, 2, 3):
                    to_x = lax.rem(x_at + dx, 4)
                    ok = to_x != y_at
                    if dx == 4 and dy == 0:
                        continue

                    @pl.when(ok)
                    def _():
                        to_plane(dy, dx, late_send, late_recv).start()

    with jax.named_scope("merge"):
        lane = lax.broadcasted_iota(jnp.int32, (1, 128), 1)
        m = parts[pl.ds(6, n_sp, stride=16), :]
        l = parts[pl.ds(7, n_sp, stride=16), :]
        top = jnp.maximum(jnp.max(m, axis=0, keepdims=True), m_new)
        f = jnp.exp(m - top)
        f_new = jnp.exp(m_new - top)
        real = jnp.logical_and(lane < 16, lane % 8 < 6)
        den = jnp.where(real, jnp.sum(f * l, axis=0, keepdims=True) + f_new, 1.0)
        wt = (jnp.concatenate([f, jnp.broadcast_to(f_new, (8, 128))], axis=0) / den).T
        slot = pl.multiple_of((group * n_lines + line) * 16, 16)
        for t in range(2):
            w8 = wt[t * 8:(t + 1) * 8]
            sums = [w8[:, n_sp:n_sp + 1] * v_new[t]] + [jnp.zeros((8, 128), F32)] * 3
            for s in range(n_sp):
                sums[s % 4] += w8[:, s:s + 1] * parts[s * 16 + t * 8:s * 16 + t * 8 + 8, :]
            acc = ((sums[0] + sums[1]) + (sums[2] + sums[3])).astype(BF16).astype(F32)
            for hd in range(6):
                full[pl.ds(slot + t * 6 + hd, 1), :] = acc[hd:hd + 1, :]

    with jax.named_scope("agsend"):
        mine_rows = full.at[pl.ds(slot, AG_ROWS)]
        zs = [lax.rem(z_at + d, 4) * 16 for d in range(4)]
        ys = [lax.rem(y_at + d, 4) * 4 for d in range(4)]
        xs_ = [lax.rem(x_at + d, 4) for d in range(4)]
        for dx in QUARTERS:
            for dz, dy in [(0, 0)] * (dx > 0) + PLANE_ORDER[::-1]:
                pltpu.make_async_remote_copy(
                    src_ref=mine_rows, dst_ref=mine_rows, send_sem=ag_send, recv_sem=ag_recv.at[group],
                    device_id={"sp": zs[dz] + ys[dy] + xs_[dx]}, device_id_type=MESH).start()

    def swap(n):
        return pltpu.make_async_remote_copy(
            src_ref=prods.at[0, n], dst_ref=other.at[n], send_sem=tp_send.at[n], recv_sem=tp_recv.at[n],
            device_id={"tp": 1 - tp}, device_id_type=MESH)

    for k, dx in enumerate(QUARTERS):
        g = lax.rem(group + 4 - dx, KV)
        with jax.named_scope(f"agwait{k}"):
            n = (n_lines if dx else n_lines - 1) * AG_ROWS
            pltpu.make_async_copy(full.at[pl.ds(0, n)], full.at[pl.ds(0, n)], ag_recv.at[g]).wait()
            wo_copy(k).wait()
        with jax.named_scope(f"wout{k}"):
            left = jnp.concatenate(
                [jnp.concatenate(
                    [full[pl.ds(g * n_lines * 16 + t * 6 + hd, n_lines, stride=16), :] for t in range(2)], axis=0)
                 for hd in range(6)], axis=1).astype(BF16)
            for n in range(OWNERS):
                res = jnp.dot(left, wo_buf[g, :, n * own:(n + 1) * own], preferred_element_type=F32)
                prods[g, n] = res
                if k == KV - 1:
                    prods[0, n] = (prods[0, n] + prods[1, n]) + (prods[2, n] + prods[3, n])
                    swap(n).start()
    with jax.named_scope("finish"):
        for n in range(OWNERS):
            swap(n).wait()
            at = slice(n * own, (n + 1) * own)
            out_ref[:, at] = (h_ref[:, at].astype(F32) + (prods[0, n] + other[n])).astype(BF16)
    with jax.named_scope("drain"):
        @pl.when(jnp.logical_and(is_kv, jnp.logical_not(is_last)))
        def _():
            wait_for(2, late_recv)
            wait_for(4, early_send)
            wait_for(11, late_send)

        @pl.when(is_last)
        def _():
            wait_for(3, late_recv)
            wait_for(3, early_send)
            wait_for(12, late_send)

        @pl.when(jnp.logical_not(is_kv))
        def _():
            wait_for(3, late_recv)
            wait_for(PLANE - 1, q_send)

        for g in range(KV):
            for i in range(heads_per):
                at = (i * KV + g) * n_seq
                new_ref[at:at + n_seq, :] = recv[g * 4 + 3, :, :, i * 128:(i + 1) * 128].reshape(n_seq, 128)
        pltpu.make_async_copy(rs_others, rs_others, rs_send).wait()
        f_others = full.at[pl.ds(0, (n_sp - 1) * AG_ROWS)]
        pltpu.make_async_copy(f_others, f_others, ag_send).wait()


def cache_kernel(pos_ref, new_ref, k_ref, v_ref, h_ref, k_out, v_out, h_out, k_fix, v_fix, sem):
    n_seq, seq_local = k_ref.shape[:2]
    sp = lax.axis_index("sp")
    base = sp * seq_local
    z_at = sp // PLANE
    trio = ((k_ref, k_fix, k_out), (v_ref, v_fix, v_out))
    hidden = pltpu.make_async_copy(h_ref, h_out, sem.at[2])
    hidden.start()
    for b in range(n_seq):
        at = pos_ref[b] - base
        here = jnp.logical_and(at >= 0, at < seq_local)

        @pl.when(jnp.logical_not(here))
        def _():
            for i, (src, _, dst) in enumerate(trio):
                pltpu.make_async_copy(src.at[b], dst.at[b], sem.at[i]).start()

        @pl.when(here)
        def _():
            for i, (src, fix, dst) in enumerate(trio):
                dz = lax.rem(b % 16 // 4 + 4 - z_at, 4)
                turn = jnp.where(dz == 2, 0, jnp.where(dz == 1, 1, jnp.where(dz == 3, 2, 3)))
                row = i * KV * n_seq + turn * 8 + b // 16 * 4 + b % 4
                fix[b] = src[b]
                fix[b, at] = new_ref[pl.ds(row, KV, stride=n_seq), :].astype(BF16)
                pltpu.make_async_copy(fix.at[b], dst.at[b], sem.at[i]).start()

    for i, (src, _, dst) in enumerate(trio):
        pltpu.make_async_copy(src, dst, sem.at[i]).wait()
    hidden.wait()


def solution(mesh):
    cache_spec = P('dp', 'sp', 'tp', None)
    n_sp = mesh.shape["sp"]

    def local_step(hidden, norm_scale, w_qkv, w_out, k_cache, v_cache, positions):
        n_seq, seq_local, kv, head_dim = k_cache.shape
        d_model = hidden.shape[1]
        width = w_qkv.shape[1] // PLANE
        depth = w_out.shape[0] // kv
        vmem = pl.BlockSpec(memory_space=VMEM)
        smem = pl.BlockSpec(memory_space=pltpu.SMEM)
        hbm = pl.BlockSpec(memory_space=pltpu.HBM)
        half = head_dim // 2
        freq = np.exp(np.arange(half, dtype=np.float32) * np.float32(-2.0 * math.log(500000.0) / head_dim))
        freq = jnp.asarray(np.concatenate([freq, freq])[None].astype(np.float32))
        flat = (n_seq, seq_local * kv, head_dim)
        dma = pltpu.SemaphoreType.DMA

        h_new, new_rows = pl.pallas_call(
            step_kernel,
            out_shape=[jax.ShapeDtypeStruct((n_seq, d_model), BF16), jax.ShapeDtypeStruct((2 * kv * n_seq, head_dim), F32)],
            in_specs=[hbm] * 8,
            out_specs=[vmem, vmem],
            scratch_shapes=[
                pltpu.SMEM((n_seq,), jnp.int32),
                VMEM((n_seq, d_model), BF16),
                VMEM((d_model,), BF16),
                VMEM((1, head_dim), F32),
                dma((4,)),
                VMEM((d_model, width), BF16),
                VMEM((kv, depth, d_model), BF16),
                VMEM(flat, BF16),
                VMEM(flat, BF16),
                VMEM((PLANE, 4, 8, width), F32),
                VMEM((n_seq * 32, head_dim), F32),
                VMEM((n_seq * 32, head_dim), BF16),
                VMEM((n_sp * 16, head_dim), F32),
                VMEM((n_sp * 16, head_dim), F32),
                VMEM((n_sp * 16, head_dim), F32),
                VMEM((kv, OWNERS, n_seq, d_model // OWNERS), F32),
                VMEM((OWNERS, n_seq, d_model // OWNERS), F32),
                dma((K_CHUNKS,)), dma((kv,)), dma((2,)), dma, dma((2,)),
            ] + [dma] * 7 + [dma((kv,)), dma((OWNERS,)), dma((OWNERS,)), pltpu.SemaphoreType.REGULAR],
            compiler_params=pltpu.CompilerParams(
                collective_id=0, has_side_effects=True, vmem_limit_bytes=52 * 1024 * 1024),
            cost_estimate=pl.CostEstimate(flops=60_000_000_000, bytes_accessed=20_000_000, transcendentals=0),
            name="step",
        )(*[pltpu.with_memory_space_constraint(a, pltpu.HBM) for a in (
            positions, hidden, norm_scale, freq, w_qkv, w_out, k_cache.reshape(flat), v_cache.reshape(flat))])

        k_new, v_new, h_out = pl.pallas_call(
            cache_kernel,
            out_shape=[jax.ShapeDtypeStruct(k_cache.shape, BF16)] * 2 + [jax.ShapeDtypeStruct((n_seq, d_model), BF16)],
            in_specs=[smem, vmem, vmem, vmem, vmem],
            out_specs=[hbm, hbm, hbm],
            scratch_shapes=[VMEM(k_cache.shape, BF16)] * 2 + [dma((3,))],
            compiler_params=pltpu.CompilerParams(vmem_limit_bytes=12 * 1024 * 1024),
            name="cache",
        )(positions, new_rows, pltpu.with_memory_space_constraint(k_cache, VMEM),
          pltpu.with_memory_space_constraint(v_cache, VMEM), h_new)
        return h_out, k_new, v_new

    return jax.shard_map(
        local_step,
        mesh=mesh,
        in_specs=(P('dp', None), P(None), P(None, 'tp'), P('tp', None), cache_spec, cache_spec, P('dp')),
        out_specs=(P('dp', None), cache_spec, cache_spec),
        check_vma=False,
    )
```

time: 48.2 us -> 47.2 us (0.979)
  Pallas kernels: 47.4 us -> 46.4 us
    pallas_call x1, Pallas kernels: 44.7 us -> 43.8 us  [local_step(): pl.pallas_call(step_kernel, out_shape=[jax.ShapeDtypeStruct((n_seq, d_mod...]
where the time goes in v4:
time: 47.2 us; the launch traced here: 47.1 us
  Pallas kernels  46.4 us (98%)
  between operations  0.69 us (1%)
    pallas_call x1, Pallas kernels, local_step(): pl.pallas_call(step_kernel, out_shape=[jax.ShapeDtypeStruct((n_seq, d_mod...  43.8 us
    pallas_call x1, Pallas kernels, local_step(): pl.pallas_call(cache_kernel, out_shape=[jax.ShapeDtypeStruct(k_cache.shap...  2.65 us

profile of v4, /device:TPU:1, one launch (start us, length us, event | category | flops | bytes accessed | tf_op | source)
XLA Modules:
  0.0 47.1 jit_solution(14201845139776088843)
XLA Ops:
  0.6 0.0 copy-start
  0.6 0.0 copy-start.1
  0.7 0.0 copy-start.2
  0.7 43.8 %step.1 = (bf16[32,6144]{1,0:T(8,128)(2,1)S(1)}, f32[256,128]{1,0:T(8,128)S(1)}) custom-call(s32[32]{0:T(128)} %pos_ref.1, bf16[32,6144]{1,0:T(8,128)(2,1)} %h_hbm.1, bf16[6144]{0:T(1024)(128)(2,1)} %scale_hbm.1, f32[1,128]{1,0:T(1,128)} %constant.2.clone.freq_hbm, bf16[6144,4096]{1,0:T(8,128)(2,1)} %wq_ref.1, bf16[3072,6144]{1,0:T(8,128)(2,1)} %wo_ref.1, ...), custom_call_target="tpu_custom_call" | custom-call | flops 60000002048 | bytes 20000000 | tf_op jit(solution)/shard_map/step/pallas_call | solution.py:435
  44.4 0.0 copy-done
  44.4 0.0 copy-done.1
  44.5 0.0 copy-done.2
  44.5 2.6 %cache.1 = (bf16[32,64,4,128]{3,2,1,0:T(4,128)(2,1)}, bf16[32,64,4,128]{3,2,1,0:T(4,128)(2,1)}, bf16[32,6144]{1,0:T(8,128)(2,1)}) custom-call(s32[32]{0:T(128)S(1)} %copy-done.2, f32[256,128]{1,0:T(8,128)S(1)} %get-tuple-element.8.new_ref, bf16[32,64,4,128]{3,2,1,0:T(4,128)(2,1)S(1)} %copy-done, bf16[32,64,4,128]{3,2,1,0:T(4,128)(2,1)S(1)} %copy-done.1, ...), custom_call_target="tpu_custom_call" | custom-call | tf_op jit(solution)/shard_map/cache/pallas_call | solution.py:467
Async XLA Ops:
  0.6 43.8 %copy-start = (bf16[32,64,4,128]{3,2,1,0:T(4,128)(2,1)S(1)}, bf16[32,64,4,128]{3,2,1,0:T(4,128)(2,1)}, u32[]{:S(2)}) copy-start(bf16[32,64,4,128]{3,2,1,0:T(4,128)(2,1)} %k_ref.1) | copy-start | bytes 6291460
  0.6 43.8 %copy-start.1 = (bf16[32,64,4,128]{3,2,1,0:T(4,128)(2,1)S(1)}, bf16[32,64,4,128]{3,2,1,0:T(4,128)(2,1)}, u32[]{:S(2)}) copy-start(bf16[32,64,4,128]{3,2,1,0:T(4,128)(2,1)} %v_ref.1) | copy-start | bytes 6291460
  0.7 43.8 %copy-start.2 = (s32[32]{0:T(128)S(1)}, s32[32]{0:T(128)}, u32[]{:S(2)}) copy-start(s32[32]{0:T(128)} %pos_ref.1) | copy-start | bytes 388
